TPU v7x, 128 devices: a whole 4x4x4 slice. The times are simulated.
128 devices in a mesh: data: 128 (over z, y, x, core).
Axes of the slice: x: 4, y: 4, z: 4, core: 2. Of those that a mesh axis runs over, the one named last changes fastest.
Arguments:
- x_step: bfloat16 [2, 256, 196, 512], P(None, 'data')
- labels: int32 [2, 256], P(None, 'data')
- x_next: bfloat16 [256, 196, 512], P('data')
- w_in: float32 [6, 512, 2048], replicated
- w_out: float32 [6, 2048, 512], replicated
- w_head: float32 [512, 1000], replicated
- mom_in: float32 [6, 512, 2048], replicated
- mom_out: float32 [6, 2048, 512], replicated
- mom_head: float32 [512, 1000], replicated
- learn_rate: float32 [], replicated
- mom_coef: float32 [], replicated
Outputs:
- output 1: float32 [256, 1000], P('data')
- output 2: float32 [6, 512, 2048], replicated
- output 3: float32 [6, 2048, 512], replicated
- output 4: float32 [512, 1000], replicated
- output 5: float32 [6, 512, 2048], replicated
- output 6: float32 [6, 2048, 512], replicated
- output 7: float32 [512, 1000], replicated
All inputs are finite; a program needn't handle non-finite values.
Results may differ from a plain program's by a relative error of at most 0.0168491.
Values are sent between devices in bfloat16 or wider.
A program may use at most 1 GiB of HBM per device.

v0:
```python
import jax
import jax.numpy as jnp
from jax import lax
from jax.sharding import PartitionSpec as P

LN_EPS = 1e-6


def norm_rows(x_f32):
    row_mean = jnp.mean(x_f32, axis=-1, keepdims=True)
    centered = x_f32 - row_mean
    row_var = jnp.mean(centered * centered, axis=-1, keepdims=True)
    return centered * lax.rsqrt(row_var + LN_EPS)


def block_forward(tok_act, w_one, w_two):
    x_f32 = tok_act.astype(jnp.float32)
    normed = norm_rows(x_f32).astype(jnp.bfloat16)
    pre_act = jnp.einsum('bsd,df->bsf', normed, w_one, preferred_element_type=jnp.float32)
    hidden = jax.nn.gelu(pre_act).astype(jnp.bfloat16)
    mlp_out = jnp.einsum('bsf,fd->bsd', hidden, w_two, preferred_element_type=jnp.float32)
    return (x_f32 + mlp_out).astype(jnp.bfloat16), (normed, pre_act, hidden)


def block_backward(tok_act, saved_act, d_out, w_one, w_two, need_input):
    normed, pre_act, hidden = saved_act
    d_out_b = d_out.astype(jnp.bfloat16)
    g_two = jnp.einsum('bsf,bsd->fd', hidden, d_out_b, preferred_element_type=jnp.float32)
    d_hidden = jnp.einsum('bsd,fd->bsf', d_out_b, w_two, preferred_element_type=jnp.float32)
    _, gelu_back = jax.vjp(jax.nn.gelu, pre_act)
    d_pre = gelu_back(d_hidden)[0].astype(jnp.bfloat16)
    g_one = jnp.einsum('bsd,bsf->df', normed, d_pre, preferred_element_type=jnp.float32)
    if not need_input:
        return g_one, g_two, d_out
    d_normed = jnp.einsum('bsf,df->bsd', d_pre, w_one, preferred_element_type=jnp.float32)
    _, norm_back = jax.vjp(norm_rows, tok_act.astype(jnp.float32))
    return g_one, g_two, d_out + norm_back(d_normed)[0]


def head_logits(tok_act, w_head_b):
    pooled = jnp.mean(tok_act, axis=1, dtype=jnp.float32).astype(jnp.bfloat16)
    return pooled, jnp.dot(pooled, w_head_b, preferred_element_type=jnp.float32)


def head_backward(tok_act, lab_row, w_head_b, examples):
    pooled, logits = head_logits(tok_act, w_head_b)
    soft_prob = jax.nn.softmax(logits, axis=-1)
    onehot = (lab_row[:, None] == jnp.arange(logits.shape[1])[None, :]).astype(jnp.float32)
    d_logits = ((soft_prob - onehot) / examples).astype(jnp.bfloat16)
    g_head = jnp.einsum('bd,bc->dc', pooled, d_logits, preferred_element_type=jnp.float32)
    d_pooled = jnp.einsum('bc,dc->bd', d_logits, w_head_b, preferred_element_type=jnp.float32)
    d_top = jnp.broadcast_to((d_pooled / tok_act.shape[1])[:, None, :], tok_act.shape)
    return g_head, d_top


def next_logits(images, new_w_in, new_w_out, new_w_head):
    w_in_b = new_w_in.astype(jnp.bfloat16)
    w_out_b = new_w_out.astype(jnp.bfloat16)
    tok_act = images
    for layer_idx in range(new_w_in.shape[0]):
        tok_act, _ = block_forward(tok_act, w_in_b[layer_idx], w_out_b[layer_idx])
    return head_logits(tok_act, new_w_head.astype(jnp.bfloat16))[1]


def solution(mesh):
    group_size = mesh.shape['data']

    def local_step(x_step, labels, x_next, w_in, w_out, w_head, mom_in, mom_out, mom_head, learn_rate, mom_coef):
        micro_count = x_step.shape[0]
        layers = w_in.shape[0]
        examples = micro_count * x_step.shape[1] * group_size
        w_in_b = w_in.astype(jnp.bfloat16)
        w_out_b = w_out.astype(jnp.bfloat16)
        w_head_b = w_head.astype(jnp.bfloat16)
        sum_in = [None] * layers
        sum_out = [None] * layers
        red_in = [None] * layers
        red_out = [None] * layers
        sum_head = None
        red_head = None
        for step_index in range(micro_count):
            last_micro = step_index == micro_count - 1
            tok_act = x_step[step_index]
            kept_in = []
            kept_act = []
            for layer_idx in range(layers):
                kept_in.append(tok_act)
                tok_act, saved_act = block_forward(tok_act, w_in_b[layer_idx], w_out_b[layer_idx])
                kept_act.append(saved_act)
            g_head, d_act = head_backward(tok_act, labels[step_index], w_head_b, examples)
            sum_head = g_head if sum_head is None else sum_head + g_head
            if last_micro:
                red_head = lax.psum(sum_head.astype(jnp.bfloat16), 'data')
            for layer_idx in reversed(range(layers)):
                g_one, g_two, d_act = block_backward(kept_in[layer_idx], kept_act[layer_idx], d_act, w_in_b[layer_idx], w_out_b[layer_idx], layer_idx > 0)
                sum_out[layer_idx] = g_two if sum_out[layer_idx] is None else sum_out[layer_idx] + g_two
                sum_in[layer_idx] = g_one if sum_in[layer_idx] is None else sum_in[layer_idx] + g_one
                if last_micro:
                    red_out[layer_idx] = lax.psum(sum_out[layer_idx].astype(jnp.bfloat16), 'data')
                    red_in[layer_idx] = lax.psum(sum_in[layer_idx].astype(jnp.bfloat16), 'data')
        new_mom_in = mom_coef * mom_in + jnp.stack(red_in).astype(jnp.float32)
        new_mom_out = mom_coef * mom_out + jnp.stack(red_out).astype(jnp.float32)
        new_mom_head = mom_coef * mom_head + red_head.astype(jnp.float32)
        new_w_in = w_in - learn_rate * new_mom_in
        new_w_out = w_out - learn_rate * new_mom_out
        new_w_head = w_head - learn_rate * new_mom_head
        logits_next = next_logits(x_next, new_w_in, new_w_out, new_w_head)
        return (logits_next, new_w_in, new_w_out, new_w_head, new_mom_in, new_mom_out, new_mom_head)

    return jax.shard_map(local_step, mesh=mesh, in_specs=(P(None, 'data', None, None), P(None, 'data'), P('data', None, None), P(), P(), P(), P(), P(), P(), P(), P()), out_specs=(P('data', None), P(), P(), P(), P(), P(), P()), check_vma=False)
```

profile of v0, /device:TPU:1, one launch (start us, length us, event | category | flops | bytes accessed | tf_op | source)
XLA Modules:
  0.0 624.9 jit_solution(4154831444561350555)
XLA Ops:
  7.2 10.2 %convert_element_type.421 = bf16[6,512,2048]{2,1,0:T(8,128)(2,1)S(1)} convert(f32[6,512,2048]{2,1,0:T(8,128)} %param.14) | non-fusion elementwise | flops 6291456 | bytes 37748736 | tf_op jit(solution)/shard_map/convert_element_type | solution.py:72
  18.5 9.1 %copy-done.1 = f32[6,2048,512]{2,1,0:T(8,128)S(1)} copy-done((f32[6,2048,512]{2,1,0:T(8,128)S(1)}, f32[6,2048,512]{2,1,0:T(8,128)}, u32[]{:S(2)}) %copy-start.1) | copy-done | bytes 25165848
  27.6 5.5 convert_element_type.423
  34.3 4.3 fusion.433
  58.2 4.2 fusion.53
  67.5 3.8 fusion.46
  71.3 4.9 fusion.360
  105.9 4.2 fusion.95
  111.7 4.6 fusion.88
  162.2 8.7 %fusion.164 = f32[512,2048,1]{1,0,2:T(8,128)} fusion(f32[2,196,2048]{2,1,0:T(8,128)} %copy-done.44, bf16[2,196,512]{2,1,0:T(8,128)(2,1)} %add_convert_fusion.2, bf16[6,2048,512]{2,1,0:T(8,128)(2,1)} %convert_element_type.423, f32[2,196]{1,0:T(2,128)S(1)} %copy-done.78, f32[2,196]{1,0:T(2,128)S(1)} %copy-done.72, bf16[1,2,196,512]{3,1,2,0:T(2,128)(2,1)} %copy-done.19), kind=kOutput, calls=%fused_computation.249 | convolution fusion | flops 1661026304 | bytes 10382400 | tf_op jit(solution)/shard_map/bsd,bsf->df/dot_general | solution.py:32
  170.9 5.7 fusion.424
  188.0 4.2 fusion.74
  199.9 4.2 fusion.67
  229.1 7.4 %fusion.144 = bf16[1,512,2048]{2,1,0:T(8,128)(2,1)} fusion(f32[512,2048,1]{1,0,2:T(8,128)} %fusion.164, f32[2,196,2048]{2,1,0:T(8,128)} %copy-done.45, bf16[2,196,512]{2,1,0:T(8,128)(2,1)S(1)} %add_convert_fusion.1, bf16[6,2048,512]{2,1,0:T(8,128)(2,1)} %convert_element_type.423, f32[2,196]{1,0:T(2,128)S(1)} %copy-done.80, f32[2,196]{1,0:T(2,128)S(1)} %copy-done.74, ...), kind=kOutput, calls=%fused_computation.202 | convolution fusion | flops 1663123456 | bytes 12471360 | tf_op jit(solution)/shard_map/bsd,bsf->df/dot_general | solution.py:32
  236.5 6.2 fusion.150
  246.1 246.1 %all-reduce.3.cloned.1.call-done = (bf16[512,1000]{0,1:T(8,128)(2,1)}, bf16[1,2048,512]{2,1,0:T(8,128)(2,1)}, bf16[1,2048,512]{2,1,0:T(8,128)(2,1)}, bf16[1,2048...) async-done(((bf16[512,1000]{0,1:T(8,128)(2,1)}, ...) | async-done | bytes 26189840 | tf_op jit(solution)/shard_map/psum | solution.py:93
  506.7 39.4 %fusion.426 = (bf16[6,512,2048]{2,1,0:T(8,128)(2,1)}, f32[6,512,2048]{2,1,0:T(8,128)}, f32[6,512,2048]{2,1,0:T(8,128)}) fusion(f32[6,512,2048]{2,1,0:T(8,128)} %param.14, f32[]{:T(128)S(6)} %copy.77, bf16[6,512,2048]{2,1,0:T(8,128)(2,1)} %copy-done.2, f32[6,512,2048]{2,1,0:T(8,128)} %param.17, f32[]{:T(128)S(6)} %copy.78), kind=kLoop, calls=%fused_computation.639 | loop fusion | flops 37748736 | bytes 125829128 | tf_op jit(solution)/shard_map/convert_element_type | solution.py:57
  546.2 36.3 %fusion.427 = (bf16[6,2048,512]{2,1,0:T(8,128)(2,1)}, f32[6,2048,512]{2,1,0:T(8,128)}, f32[6,2048,512]{2,1,0:T(8,128)}) fusion(f32[6,2048,512]{2,1,0:T(8,128)} %param.15, f32[]{:T(128)S(6)} %copy.77, bf16[6,2048,512]{2,1,0:T(8,128)(2,1)S(1)} %constant_dynamic-update-slice_fusion.6, f32[6,2048,512]{2,1,0:T(8,128)} %param.18, f32[]{:T(128)S(6)} %copy.78), kind=kLoop, calls=%fused_computation.640 | loop fusion | flops 37748736 | bytes 125829128 | tf_op jit(solution)/shard_map/convert_element_type | solution.py:58
  582.5 4.6 fusion.447
  587.4 4.6 fusion.450
  592.3 4.6 fusion.451
  597.2 4.6 fusion.452
  602.1 4.6 fusion.453
  607.6 5.1 fusion.265
  (373 shorter events, 170.7 us)
Async XLA Ops:
  7.2 10.3 %copy-start.68 = (bf16[2,2,196,512]{3,1,2,0:T(2,128)(2,1)S(1)}, bf16[2,2,196,512]{3,1,2,0:T(2,128)(2,1)}, u32[]{:S(2)}) copy-start(bf16[2,2,196,512]{3,1,2,0:T(2,128)(2,1)} %param.11) | copy-start | bytes 2408452
  7.2 485.0 %all-reduce.3.cloned.1.call-start = ((), (), s32[]{:S(2)}) async-start(), calls=%async_computation | async-start | bytes 52379648 | tf_op jit(solution)/shard_map/psum | solution.py:93
  7.2 20.4 %copy-start.1 = (f32[6,2048,512]{2,1,0:T(8,128)S(1)}, f32[6,2048,512]{2,1,0:T(8,128)}, u32[]{:S(2)}) copy-start(f32[6,2048,512]{2,1,0:T(8,128)} %param.15) | copy-start | bytes 75497472
  17.4 123.8 %copy-start = (bf16[6,512,2048]{2,1,0:T(8,128)(2,1)}, bf16[6,512,2048]{2,1,0:T(8,128)(2,1)S(1)}, u32[]{:S(2)}) copy-start(bf16[6,512,2048]{2,1,0:T(8,128)(2,1)S(1)} %convert_element_type.421) | copy-start | bytes 37748740
  18.0 16.2 %copy-start.19 = (bf16[1,2,196,512]{3,1,2,0:T(2,128)(2,1)}, bf16[1,2,196,512]{3,1,2,0:T(2,128)(2,1)S(1)}, u32[]{:S(2)}) copy-start(bf16[1,2,196,512]{3,1,2,0:T(2,128)(2,1)S(1)} %get-tuple-element.37) | copy-start | bytes 1204228
  18.0 70.0 %copy-start.17 = (bf16[1,2,196,512]{3,1,2,0:T(2,128)(2,1)}, bf16[1,2,196,512]{3,1,2,0:T(2,128)(2,1)S(1)}, u32[]{:S(2)}) copy-start(bf16[1,2,196,512]{3,1,2,0:T(2,128)(2,1)S(1)} %get-tuple-element.36) | copy-start | bytes 1204228
  18.2 14.9 %copy-start.71 = (f32[2,196]{1,0:T(2,128)}, f32[2,196]{1,0:T(2,128)S(1)}, u32[]{:S(2)}) copy-start(f32[2,196]{1,0:T(2,128)S(1)} %broadcast_multiply_fusion.16) | copy-start | bytes 4708
  33.1 6.8 %slice-start = ((s8[12582912]{0:T(1024)(128)(4,1)}), s8[4194304]{0:T(1024)(128)(4,1)S(1)}, s32[]{:S(2)}) async-start(s8[12582912]{0:T(1024)(128)(4,1)} %bitcast.534), calls=%async_computation.1 | async-start | bytes 8388608
  46.2 32.0 %copy-start.29 = (f32[2,196,2048]{2,1,0:T(8,128)}, f32[2,196,2048]{2,1,0:T(8,128)S(1)}, u32[]{:S(2)}) copy-start(f32[2,196,2048]{2,1,0:T(8,128)S(1)} %fusion.194) | copy-start | bytes 9633796
  48.9 18.6 %copy-start.33 = (f32[2,196,2048]{2,1,0:T(8,128)}, f32[2,196,2048]{2,1,0:T(8,128)S(1)}, u32[]{:S(2)}) copy-start(f32[2,196,2048]{2,1,0:T(8,128)S(1)} %fusion.200) | copy-start | bytes 9633796
  67.5 10.3 %copy-start.42 = (f32[2,196,512]{2,1,0:T(8,128)}, f32[2,196,512]{2,1,0:T(8,128)S(1)}, u32[]{:S(2)}) copy-start(f32[2,196,512]{2,1,0:T(8,128)S(1)} %get-tuple-element.31) | copy-start | bytes 2408452
  97.3 21.0 %copy-start.31 = (f32[2,196,2048]{2,1,0:T(8,128)}, f32[2,196,2048]{2,1,0:T(8,128)S(1)}, u32[]{:S(2)}) copy-start(f32[2,196,2048]{2,1,0:T(8,128)S(1)} %fusion.192) | copy-start | bytes 9633796
  101.9 9.4 %copy-start.8 = (f32[2,196,512]{2,1,0:T(8,128)}, f32[2,196,512]{2,1,0:T(8,128)S(1)}, u32[]{:S(2)}) copy-start(f32[2,196,512]{2,1,0:T(8,128)S(1)} %get-tuple-element.61) | copy-start | bytes 2408452
  111.7 6.2 copy-start.40
  170.9 5.7 copy-start.70
  170.9 5.7 copy-start.82
  170.9 5.7 copy-start.84
  170.9 5.7 copy-start.86
  170.9 5.7 copy-start.88
  170.9 7.6 %copy-start.3 = (f32[512,2048,1]{1,0,2:T(8,128)S(1)}, f32[512,2048,1]{1,0,2:T(8,128)}, u32[]{:S(2)}) copy-start(f32[512,2048,1]{1,0,2:T(8,128)} %fusion.361) | copy-start | bytes 12582916
  170.9 7.6 %copy-start.9 = (f32[2,196,512]{2,1,0:T(8,128)S(1)}, f32[2,196,512]{2,1,0:T(8,128)}, u32[]{:S(2)}) copy-start(f32[2,196,512]{2,1,0:T(8,128)} %copy-done.8) | copy-start | bytes 2408452
  170.9 7.6 %copy-start.59 = (bf16[2,196,2048]{2,1,0:T(8,128)(2,1)S(1)}, bf16[2,196,2048]{2,1,0:T(8,128)(2,1)}, u32[]{:S(2)}) copy-start(bf16[2,196,2048]{2,1,0:T(8,128)(2,1)} %copy-done.58) | copy-start | bytes 4816900
  236.5 6.2 copy-start.10
  498.8 6.9 %copy-start.2 = (bf16[6,512,2048]{2,1,0:T(8,128)(2,1)}, bf16[6,512,2048]{2,1,0:T(8,128)(2,1)S(1)}, u32[]{:S(2)}) copy-start(bf16[6,512,2048]{2,1,0:T(8,128)(2,1)S(1)} %constant_dynamic-update-slice_fusion) | copy-start | bytes 37748740
  (75 other events, 221.4 us)
Sparse Core Ops, SparseCore 0:
  244.4 247.7 all-reduce.2
where the time goes:
time: 635 us; the launch traced here: 625 us
  waiting for transfers between devices  246 us (39%)
  matrix products  217 us (34%)
  other arithmetic  109 us (17%)
  local copies, waits for them, and re-layouts  35.4 us (6%)
  between operations  16.9 us (3%)
    psum x1, waiting for transfers between devices, local_step(): red_head = lax.psum(sum_head.astype(jnp.bfloat16), 'data')  246 us
    dot_general x18, matrix products, block_forward(): jnp.einsum('bsf,fd->bsd', hidden, w_two, preferred_element_type=jnp.float32)  49.5 us
    dot_general x12, matrix products, block_backward(): jnp.einsum('bsd,bsf->df', normed, d_pre, preferred_element_type=jnp.float32)  48.7 us
    dot_general x12, matrix products, block_backward(): jnp.einsum('bsf,bsd->fd', hidden, d_out_b, preferred_element_type=jnp.flo...  44.8 us
    convert_element_type x1, other arithmetic, next_logits(): w_in_b = new_w_in.astype(jnp.bfloat16)  39.4 us
    dot_general x10, matrix products, block_backward(): jnp.einsum('bsd,fd->bsf', d_out_b, w_two, preferred_element_type=jnp.floa...  37.2 us
    convert_element_type x1, other arithmetic, next_logits(): w_out_b = new_w_out.astype(jnp.bfloat16)  36.3 us
    unnamed x206, local copies, waits for them, and re-layouts  34.5 us
  transfers between devices with their start and end apart: 1, of which 1 were waited for; matrix products, arithmetic and copies ran while one was open for 0% of the time, Pallas kernels for 0%

commit v1 on v0

v1 whole, which is shorter than its diff:
```python
import functools

import jax
import jax.numpy as jnp
from jax import lax
from jax.experimental import pallas as pl
from jax.experimental.pallas import tpu as pltpu
from jax.sharding import PartitionSpec as P

LN_EPS = 1e-6
GELU_A = 0.7978845608028654
GELU_B = 0.044715
CHUNK = 512
LANES = 256
MESH_ID = pl.DeviceIdType.MESH
F32 = jnp.float32
BF16 = jnp.bfloat16


def norm_parts(x_f32):
    row_mean = jnp.mean(x_f32, axis=-1, keepdims=True)
    centered = x_f32 - row_mean
    row_var = jnp.mean(centered * centered, axis=-1, keepdims=True)
    inv = lax.rsqrt(row_var + LN_EPS)
    return centered * inv, inv


def gelu_tanh(pre):
    th = jnp.tanh(GELU_A * (pre + GELU_B * (pre * pre * pre)))
    return 0.5 * pre * (1.0 + th), th


def mm(a, b, dims=((1,), (0,))):
    return lax.dot_general(a, b, (dims, ((), ())), preferred_element_type=F32)


def cost(flops, bytes_accessed):
    return pl.CostEstimate(flops=flops, bytes_accessed=bytes_accessed, transcendentals=0)


def fwd_body(n_chunk, x0_ref, w1_ref, w2_ref, xs_ref, pre_ref, y_ref, x_s, n_s, acc_s):
    layer, step = pl.program_id(0), pl.program_id(1)

    @pl.when((layer == 0) & (step == 0))
    def _():
        x_s[...] = x0_ref[...]

    @pl.when(step == 0)
    def _():
        x_f32 = x_s[...].astype(F32)
        n_s[...] = norm_parts(x_f32)[0].astype(BF16)
        acc_s[...] = x_f32
        xs_ref[0] = x_s[...]

    pre = mm(n_s[...], w1_ref[0].astype(BF16))
    pre_ref[0] = pre
    hidden = gelu_tanh(pre)[0].astype(BF16)
    acc_s[...] += mm(hidden, w2_ref[0].astype(BF16))

    @pl.when(step == n_chunk - 1)
    def _():
        out = acc_s[...].astype(BF16)
        x_s[...] = out
        y_ref[...] = out


def forward(x0, w_in, w_out):
    layers, d, ff = w_in.shape
    rows = x0.shape[0]
    n_chunk = ff // CHUNK
    return pl.pallas_call(
        functools.partial(fwd_body, n_chunk),
        grid=(layers, n_chunk),
        in_specs=[
            pl.BlockSpec((rows, d), lambda l, j: (0, 0)),
            pl.BlockSpec((1, d, CHUNK), lambda l, j: (l, 0, j)),
            pl.BlockSpec((1, CHUNK, d), lambda l, j: (l, j, 0)),
        ],
        out_specs=[
            pl.BlockSpec((1, rows, d), lambda l, j: (l, 0, 0)),
            pl.BlockSpec((1, rows, CHUNK), lambda l, j: (l, 0, j)),
            pl.BlockSpec((rows, d), lambda l, j: (0, 0)),
        ],
        out_shape=[
            jax.ShapeDtypeStruct((layers, rows, d), BF16),
            jax.ShapeDtypeStruct((layers, rows, ff), F32),
            jax.ShapeDtypeStruct((rows, d), BF16),
        ],
        scratch_shapes=[pltpu.VMEM((rows, d), BF16), pltpu.VMEM((rows, d), BF16), pltpu.VMEM((rows, d), F32)],
        cost_estimate=cost(4 * layers * rows * d * ff, 8 * layers * d * ff + 4 * layers * rows * ff),
        compiler_params=pltpu.CompilerParams(vmem_limit_bytes=48 << 20),
        name="mlp_forward",
    )(x0, w_in, w_out)


def bwd_body(n_chunk, dtop_ref, xs_ref, pre_ref, w1_ref, w2_ref, g1_ref, g2_ref, dx_ref, d_s, db_s, n_s, dn_s):
    layer, step = pl.program_id(0), pl.program_id(1)

    @pl.when((layer == 0) & (step == 0))
    def _():
        d_s[...] = dtop_ref[...]

    @pl.when(step == 0)
    def _():
        db_s[...] = d_s[...].astype(BF16)
        n_s[...] = norm_parts(xs_ref[0].astype(F32))[0].astype(BF16)
        dn_s[...] = jnp.zeros_like(dn_s)

    pre = pre_ref[0]
    half_out, th = gelu_tanh(pre)
    hidden = half_out.astype(BF16)
    slope = 0.5 * (1.0 + th) + (0.5 * GELU_A) * pre * (1.0 - th * th) * (1.0 + (3.0 * GELU_B) * (pre * pre))
    d_b = db_s[...]
    d_hidden = mm(d_b, w2_ref[0].astype(BF16), ((1,), (1,)))
    d_pre = (slope * d_hidden).astype(BF16)
    g_two = mm(hidden, d_b, ((0,), (0,))).astype(BF16)
    g_one = mm(n_s[...], d_pre, ((0,), (0,))).astype(BF16)
    for part in range(2):
        g1_ref[0, part] = g_one[:, part * LANES:(part + 1) * LANES]
        g2_ref[0, part, 0] = g_two[:, part * LANES:(part + 1) * LANES]
    dn_s[...] += mm(d_pre, w1_ref[0].astype(BF16), ((1,), (1,)))

    @pl.when(step == n_chunk - 1)
    def _():
        normed, inv = norm_parts(xs_ref[0].astype(F32))
        dn = dn_s[...]
        along = jnp.mean(dn * normed, axis=-1, keepdims=True)
        out = d_s[...] + inv * (dn - jnp.mean(dn, axis=-1, keepdims=True) - normed * along)
        d_s[...] = out
        dx_ref[...] = out


def backward(d_top, xs, pre, w_in, w_out, first, count):
    _, d, ff = w_in.shape
    rows = d_top.shape[0]
    n_chunk = ff // CHUNK
    return pl.pallas_call(
        functools.partial(bwd_body, n_chunk),
        grid=(count, n_chunk),
        in_specs=[
            pl.BlockSpec((rows, d), lambda l, j: (0, 0)),
            pl.BlockSpec((1, rows, d), lambda l, j: (first - l, 0, 0)),
            pl.BlockSpec((1, rows, CHUNK), lambda l, j: (first - l, 0, j)),
            pl.BlockSpec((1, d, CHUNK), lambda l, j: (first - l, 0, j)),
            pl.BlockSpec((1, CHUNK, d), lambda l, j: (first - l, j, 0)),
        ],
        out_specs=[
            pl.BlockSpec((1, 2, d, LANES), lambda l, j: (first - l, j, 0, 0)),
            pl.BlockSpec((1, 2, 1, CHUNK, LANES), lambda l, j: (first - l, 0, j, 0, 0)),
            pl.BlockSpec((rows, d), lambda l, j: (0, 0)),
        ],
        out_shape=[
            jax.ShapeDtypeStruct((count, 2 * n_chunk, d, LANES), BF16),
            jax.ShapeDtypeStruct((count, 2, n_chunk, CHUNK, LANES), BF16),
            jax.ShapeDtypeStruct((rows, d), F32),
        ],
        scratch_shapes=[
            pltpu.VMEM((rows, d), F32),
            pltpu.VMEM((rows, d), BF16),
            pltpu.VMEM((rows, d), BF16),
            pltpu.VMEM((rows, d), F32),
        ],
        cost_estimate=cost(8 * count * rows * d * ff, count * (12 * d * ff + 4 * rows * ff)),
        compiler_params=pltpu.CompilerParams(vmem_limit_bytes=56 << 20),
        name="mlp_backward",
    )(d_top, xs, pre, w_in, w_out)


def next_body(n_chunk, n_prev, coef_ref, x0_ref, w1_ref, m1_ref, g1_ref, w2_ref, m2_ref, g2_ref, *rest):
    rest = rest[n_prev:]
    nw1_ref, nm1_ref, nw2_ref, nm2_ref, y_ref, x_s, n_s, acc_s = rest
    layer, step = pl.program_id(0), pl.program_id(1)
    rate, momentum = coef_ref[0], coef_ref[1]

    @pl.when((layer == 0) & (step == 0))
    def _():
        x_s[...] = x0_ref[...]

    @pl.when(step == 0)
    def _():
        x_f32 = x_s[...].astype(F32)
        n_s[...] = norm_parts(x_f32)[0].astype(BF16)
        acc_s[...] = x_f32

    g_one = jnp.concatenate([g1_ref[0, 0], g1_ref[0, 1]], axis=1)
    g_two = jnp.concatenate([g2_ref[0, 0, 0], g2_ref[0, 1, 0]], axis=1)
    m1 = momentum * m1_ref[0] + g_one.astype(F32)
    w1 = w1_ref[0] - rate * m1
    nm1_ref[0] = m1
    nw1_ref[0] = w1
    m2 = momentum * m2_ref[0] + g_two.astype(F32)
    w2 = w2_ref[0] - rate * m2
    nm2_ref[0] = m2
    nw2_ref[0] = w2
    pre = mm(n_s[...], w1.astype(BF16))
    hidden = gelu_tanh(pre)[0].astype(BF16)
    acc_s[...] += mm(hidden, w2.astype(BF16))

    @pl.when(step == n_chunk - 1)
    def _():
        out = acc_s[...].astype(BF16)
        x_s[...] = out
        y_ref[...] = out


def update_forward(coef, x0, w_in, mom_in, g_in, w_out, mom_out, g_out, first, count, prev):
    layers, d, ff = w_in.shape
    rows = x0.shape[0]
    n_chunk = ff // CHUNK
    in_block = pl.BlockSpec((1, d, CHUNK), lambda l, j: (first + l, 0, j))
    out_block = pl.BlockSpec((1, CHUNK, d), lambda l, j: (first + l, j, 0))
    n_prev = 0 if prev is None else 4
    return pl.pallas_call(
        functools.partial(next_body, n_chunk, n_prev),
        grid=(count, n_chunk),
        in_specs=[
            pl.BlockSpec(memory_space=pltpu.SMEM),
            pl.BlockSpec((rows, d), lambda l, j: (0, 0)),
            in_block,
            in_block,
            pl.BlockSpec((1, 2, d, LANES), lambda l, j: (l, j, 0, 0)),
            out_block,
            out_block,
            pl.BlockSpec((1, 2, 1, CHUNK, LANES), lambda l, j: (l, 0, j, 0, 0)),
        ] + [pl.BlockSpec(memory_space=pl.ANY)] * n_prev,
        out_specs=[in_block, in_block, out_block, out_block, pl.BlockSpec((rows, d), lambda l, j: (0, 0))],
        out_shape=[
            jax.ShapeDtypeStruct(w_in.shape, F32),
            jax.ShapeDtypeStruct(w_in.shape, F32),
            jax.ShapeDtypeStruct(w_out.shape, F32),
            jax.ShapeDtypeStruct(w_out.shape, F32),
            jax.ShapeDtypeStruct((rows, d), BF16),
        ],
        scratch_shapes=[pltpu.VMEM((rows, d), BF16), pltpu.VMEM((rows, d), BF16), pltpu.VMEM((rows, d), F32)],
        input_output_aliases={8 + i: i for i in range(n_prev)},
        cost_estimate=cost(4 * count * rows * d * ff, 36 * count * d * ff),
        compiler_params=pltpu.CompilerParams(vmem_limit_bytes=48 << 20),
        name="update_forward",
    )(coef, x0, w_in, mom_in, g_in, w_out, mom_out, g_out, *(prev or ()))


def sum_body(n, layers, g1_ref, g2_ref, o1_ref, o2_ref, work, land0, land1, land2, land3,
             load_sem, d0_send, d0_recv, ring_send, ring_recv, d1_send, d1_recv, out_sem):
    rows = work.shape[2]
    sub = (rows, rows // n, rows // (n * n))
    me = lax.axis_index('data')
    core = lax.rem(me, 2)
    partner = me + 1 - 2 * core
    own, other = core * n, (1 - core) * n
    strides = (2, 2 * n, 2 * n * n)
    pos = [lax.rem(lax.div(me, stride), n) for stride in strides]
    last = n - 1
    messages = 6 * last

    def neighbour(axis, way):
        return me + (lax.rem(pos[axis] + way + n, n) - pos[axis]) * strides[axis]

    barrier = pltpu.get_barrier_semaphore()
    greeted = [partner] + [neighbour(axis, way) for axis in range(3) for way in (1, -1)]
    for device in greeted:
        pl.semaphore_signal(barrier, inc=1, device_id=(device,), device_id_type=MESH_ID)
    pl.semaphore_wait(barrier, len(greeted))

    def each(fn):
        @pl.loop(0, layers // 3)
        def _(i):
            for colour in range(3):
                for kind in range(2):
                    way = 1 - 2 * lax.rem(i, 2)
                    way = way if kind == 0 else -way
                    layer = colour + 3 * i
                    fn((g1_ref, g2_ref)[kind], (o1_ref, o2_ref)[kind], kind * layers + layer, layer, colour, way)

    def at(base, way, steps):
        return lax.rem(base - way * steps + 2 * n, n)

    def remote(src, dst, send, recv, device):
        return pltpu.make_async_remote_copy(src_ref=src, dst_ref=dst, send_sem=send, recv_sem=recv, device_id=(device,), device_id_type=MESH_ID)

    def load_copy(g_ref, m, layer, block, k):
        return pltpu.make_async_copy(g_ref.at[layer, own + block], work.at[m, own + block], load_sem.at[m, k])

    def swap_copy(g_ref, m, layer, block, k):
        return remote(g_ref.at[layer, other + block], land0.at[m, block], d0_send.at[m, k], d0_recv.at[m, k], partner)

    def share_copy(m, block, k, half):
        return remote(work.at[m, half + block], work.at[m, half + block], d1_send.at[m], d1_recv.at[m, k], partner)

    def place(m, colour, way, stage):
        block = at(pos[colour], way, last)
        row = 0
        if stage == 3:
            row = at(pos[(colour + 1) % 3], way, last) * sub[1]
        return block, row

    def piece(m, colour, way, stage, index):
        if stage == 1:
            return work.at[m, own + index]
        block, row = place(m, colour, way, stage)
        return work.at[m, own + block, pl.ds(pl.multiple_of(row + index * sub[stage - 1], sub[stage - 1]), sub[stage - 1])]

    lands = (None, land1, land2, land3)

    def message(t, m, colour, way):
        phase, s = divmod(t, last)
        stage = (1, 2, 3, 3, 2, 1)[phase]
        axis = (colour + stage - 1) % 3
        to = neighbour(axis, way)
        if phase < 3:
            src = piece(m, colour, way, stage, at(pos[axis], way, s))
            dst = lands[stage].at[m, s]
        else:
            src = piece(m, colour, way, stage, at(pos[axis], way, last + s))
            dst = src
        return remote(src, dst, ring_send.at[m], ring_recv.at[m, t], to)

    def arrival(t, m, colour, way):
        phase, s = divmod(t, last)
        stage = (1, 2, 3, 3, 2, 1)[phase]
        axis = (colour + stage - 1) % 3
        if phase < 3:
            dst = lands[stage].at[m, s]
        else:
            dst = piece(m, colour, way, stage, at(pos[axis], way, last + s + 1))
        return remote(dst, dst, ring_send.at[m], ring_recv.at[m, t], neighbour(axis, way))

    def accumulate(dst, sources):
        count = dst.shape[0]
        step = min(count, 64)

        @pl.loop(0, count // step)
        def _(r):
            part = pl.ds(pl.multiple_of(r * step, step), step)
            total = dst[part, :].astype(F32)
            for source in sources:
                total = total + source[part, :].astype(F32)
            dst[part, :] = total.astype(BF16)

    for k in range(n):
        def begin(g_ref, o_ref, m, layer, colour, way, k=k):
            block = at(pos[colour], way, k)
            swap_copy(g_ref, m, layer, block, k).start()
            load_copy(g_ref, m, layer, block, k).start()
        each(begin)

    for t in range(messages + 1):
        def tick(g_ref, o_ref, m, layer, colour, way, t=t):
            if t > 0:
                arrival(t - 1, m, colour, way).wait_recv()
                message(t - 1, m, colour, way).wait_send()
            if t <= last:
                block = at(pos[colour], way, t)
                load_copy(g_ref, m, layer, block, t).wait()
                swap_copy(g_ref, m, layer, block, t).wait_recv()
                sources = [land0.at[m, block]] + ([land1.at[m, t - 1]] if t > 0 else [])
                accumulate(work.at[m, own + block], sources)
            elif t <= 3 * last:
                phase, s = divmod(t - 1, last)
                axis = (colour + phase) % 3
                accumulate(piece(m, colour, way, phase + 1, at(pos[axis], way, s + 1)), [lands[phase + 1].at[m, s]])
            if t < messages:
                message(t, m, colour, way).start()
            k = t - 5 * last
            if k >= 0:
                if k > 0:
                    share_copy(m, at(pos[colour], way, last + k - 1), k - 1, own).wait_send()
                share_copy(m, at(pos[colour], way, last + k), k, own).start()
        each(tick)

    def finish(g_ref, o_ref, m, layer, colour, way):
        share_copy(m, at(pos[colour], way, last + last), last, own).wait_send()
        for k in range(n):
            share_copy(m, at(pos[colour], way, last + k), k, other).wait_recv()
            swap_copy(g_ref, m, layer, at(pos[colour], way, k), k).wait_send()
        pltpu.make_async_copy(work.at[m], o_ref.at[layer], out_sem.at[m]).start()
    each(finish)

    def drain(g_ref, o_ref, m, layer, colour, way):
        pltpu.make_async_copy(work.at[m], o_ref.at[layer], out_sem.at[m]).wait()
    each(drain)


def sum_gradients(g1, g2, group_size):
    n = round((group_size // 2) ** (1 / 3))
    layers, blocks, rows, lanes = g1.shape
    count = 2 * layers
    dma = pltpu.SemaphoreType.DMA
    messages = 6 * (n - 1)
    return pl.pallas_call(
        functools.partial(sum_body, n, layers),
        in_specs=[pl.BlockSpec(memory_space=pl.ANY)] * 2,
        out_specs=[pl.BlockSpec(memory_space=pl.ANY)] * 2,
        out_shape=[jax.ShapeDtypeStruct(g1.shape, BF16), jax.ShapeDtypeStruct(g2.shape, BF16)],
        scratch_shapes=[
            pltpu.VMEM((count, blocks, rows, lanes), BF16),
            pltpu.VMEM((count, n, rows, lanes), BF16),
            pltpu.VMEM((count, n - 1, rows, lanes), BF16),
            pltpu.VMEM((count, n - 1, rows // n, lanes), BF16),
            pltpu.VMEM((count, n - 1, rows // (n * n), lanes), BF16),
            dma((count, n)),
            dma((count, n)),
            dma((count, n)),
            dma((count,)),
            dma((count, messages)),
            dma((count,)),
            dma((count, n)),
            dma((count,)),
        ],
        cost_estimate=cost(1 << 30, 4 * g1.size),
        compiler_params=pltpu.CompilerParams(collective_id=0, has_side_effects=True, vmem_limit_bytes=58 << 20),
        name="gradient_sum",
    )(g1, g2)


def pool(tok_act, images):
    return jnp.mean(tok_act.reshape(images, -1, tok_act.shape[-1]), axis=1, dtype=F32).astype(BF16)


def head_backward(tok_act, lab_row, w_head_b, examples):
    images = lab_row.shape[0]
    seq = tok_act.shape[0] // images
    pooled = pool(tok_act, images)
    logits = jnp.dot(pooled, w_head_b, preferred_element_type=F32)
    soft_prob = jax.nn.softmax(logits, axis=-1)
    onehot = (lab_row[:, None] == jnp.arange(logits.shape[1])[None, :]).astype(F32)
    d_logits = ((soft_prob - onehot) / examples).astype(BF16)
    g_head = jnp.einsum('bd,bc->dc', pooled, d_logits, preferred_element_type=F32)
    d_pooled = jnp.einsum('bc,dc->bd', d_logits, w_head_b, preferred_element_type=F32)
    d_top = jnp.broadcast_to((d_pooled / seq)[:, None, :], (images, seq, tok_act.shape[1]))
    return g_head, d_top.reshape(tok_act.shape)


def solution(mesh):
    group_size = mesh.shape['data']

    def local_step(x_step, labels, x_next, w_in, w_out, w_head, mom_in, mom_out, mom_head, learn_rate, mom_coef):
        micro_count, images, seq, d = x_step.shape
        layers = w_in.shape[0]
        examples = micro_count * images * group_size
        xs, pre, top = forward(x_step.reshape(-1, d), w_in, w_out)
        w_head_b = w_head.astype(BF16)
        g_head, d_act = head_backward(top, labels.reshape(-1), w_head_b, examples)
        red_head = lax.psum(g_head.astype(BF16), 'data')
        g_in, g_out, _ = backward(d_act, xs, pre, w_in, w_out, layers - 1, layers)
        block_shape = (layers, -1) + g_out.shape[3:]
        red_in, red_out = sum_gradients(g_in, g_out.reshape(block_shape), group_size)
        coef = jnp.stack([learn_rate, mom_coef])
        tok = x_next.reshape(-1, d)
        new_w_in, new_mom_in, new_w_out, new_mom_out, tok = update_forward(coef, tok, w_in, mom_in, red_in, w_out, mom_out, red_out.reshape(g_out.shape), 0, layers, None)
        new_mom_head = mom_coef * mom_head + red_head.astype(F32)
        new_w_head = w_head - learn_rate * new_mom_head
        logits_next = jnp.dot(pool(tok, images), new_w_head.astype(BF16), preferred_element_type=F32)
        return (logits_next, new_w_in, new_w_out, new_w_head, new_mom_in, new_mom_out, new_mom_head)

    return jax.shard_map(local_step, mesh=mesh, in_specs=(P(None, 'data', None, None), P(None, 'data'), P('data', None, None), P(), P(), P(), P(), P(), P(), P(), P()), out_specs=(P('data', None), P(), P(), P(), P(), P(), P()), check_vma=False)
```

time: 635 us -> 365 us (0.57); the launches traced: 625 us -> 363 us
  Pallas kernels: 0 us -> 330 us
  waiting for transfers between devices: 246 us -> 0.04 us
  matrix products: 217 us -> 3.61 us
  other arithmetic: 109 us -> 6.65 us
  local copies, waits for them, and re-layouts: 35.4 us -> 8 us
    pallas_call x0 -> x4, Pallas kernels: none -> 330 us  [the longest x1 131 us: sum_gradients(): pl.pallas_call(functools.partial(sum_body, n, layers), in_specs=[pl.Block...]
    psum x1, waiting for transfers between devices: 246 us -> 0.02 us  [local_step(): red_head = lax.psum(g_head.astype(BF16), 'data')]
    dot_general x81 -> x4, matrix products: 217 us -> 3.61 us  [the longest x1 1.56 us: head_backward(): jnp.einsum('bd,bc->dc', pooled, d_logits, preferred_element_type=F32)]
    convert_element_type x9 -> x0, other arithmetic: 93.3 us -> none  [the longest x1 39.4 us: next_logits(): w_in_b = new_w_in.astype(jnp.bfloat16)]
    unnamed x206 -> x10, local copies, waits for them, and re-layouts: 34.5 us -> 1.31 us
    reduce_sum x30 -> x2, other arithmetic: 9.45 us -> 2.79 us  [pool(): jnp.mean(tok_act.reshape(images, -1, tok_act.shape[-1]), axis=1, dtype=F32)]
  transfers between devices with their start and end apart: 1 -> 1, of which waited for: 1 -> 0; matrix products, arithmetic and copies ran while one was open for 0% -> 2% of each run, Pallas kernels for 0% -> 78%
where the time goes in v1:
time: 365 us; the launch traced here: 363 us
  Pallas kernels  330 us (90%)
  between operations  15.4 us (4%)
  local copies, waits for them, and re-layouts  8 us (2%)
  other arithmetic  6.65 us (2%)
    pallas_call x1, Pallas kernels, sum_gradients(): pl.pallas_call(functools.partial(sum_body, n, layers), in_specs=[pl.Block...  131 us
    pallas_call x1, Pallas kernels, update_forward(): pl.pallas_call(functools.partial(next_body, n_chunk, n_prev), grid=(count...  78.6 us
    pallas_call x1, Pallas kernels, backward(): pl.pallas_call(functools.partial(bwd_body, n_chunk), grid=(count, n_chunk...  74.4 us
    pallas_call x1, Pallas kernels, forward(): pl.pallas_call(functools.partial(fwd_body, n_chunk), grid=(layers, n_chun...  46 us
  transfers between devices with their start and end apart: 1, of which 0 were waited for; matrix products, arithmetic and copies ran while one was open for 2% of the time, Pallas kernels for 78%

profile of v1, /device:TPU:1, one launch (start us, length us, event | category | flops | bytes accessed | tf_op | source)
XLA Modules:
  0.0 363.4 jit_solution(4731732058904584515)
XLA Ops:
  7.2 0.0 all-reduce.2.cloned.1.call-start
  7.2 1.2 copy.21
  8.4 0.1 reshape.40.x0_ref
  8.6 46.0 %mlp_forward.1 = (bf16[6,784,512]{2,1,0:T(8,128)(2,1)}, f32[6,784,2048]{2,1,0:T(8,128)}, bf16[784,512]{1,0:T(8,128)(2,1)S(1)}) custom-call(bf16[784,512]{1,0:T(8,128)(2,1)S(1)} %reshape.40.x0_ref, f32[6,512,2048]{2,1,0:T(8,128)} %w1_ref.5, f32[6,2048,512]{2,1,0:T(8,128)} %w2_ref.5), custom_call_target="tpu_custom_call" | custom-call | flops 19730006016 | bytes 88866816 | tf_op jit(solution)/shard_map/mlp_forward/pallas_call | solution.py:71
  54.6 1.3 reshape.44
  55.9 0.1 eq.15
  56.0 1.6 reduce_sum.27
  57.6 0.5 fusion.10
  58.1 0.2 fusion.5
  58.3 1.6 convolution_convert_fusion
  59.8 0.3 convolution_multiply_fusion
  60.1 1.4 broadcast_in_dim.2
  61.5 2.7 reshape.41.dtop_ref
  65.6 0.1 reshape.39.x0_ref
  65.7 74.4 %mlp_backward.1 = (bf16[6,8,512,256]{3,2,1,0:T(8,128)(2,1)}, bf16[6,2,4,512,256]{4,3,2,1,0:T(8,128)(2,1)}, f32[784,512]{1,0:T(8,128)}) custom-call(f32[784,512]{1,0:T(8,128)} %reshape.41.dtop_ref, bf16[6,784,512]{2,1,0:T(8,128)(2,1)} %get-tuple-element.20.xs_ref, f32[6,784,2048]{2,1,0:T(8,128)} %get-tuple-element.21.pre_ref, f32[6,512,2048]{2,1,0:T(8,128)} %w1_ref.5, ...), custom_call_target="tpu_custom_call" | custom-call | flops 39460012032 | bytes 114032640 | tf_op jit(solution)/shard_map/mlp_backward/pallas_call | solution.py:137
  140.1 130.7 %gradient_sum.1 = (bf16[6,8,512,256]{3,2,1,0:T(8,128)(2,1)}, bf16[6,8,512,256]{3,2,1,0:T(8,128)(2,1)}) custom-call(bf16[6,8,512,256]{3,2,1,0:T(8,128)(2,1)} %get-tuple-element.22.g1_ref, bf16[6,8,512,256]{3,2,1,0:T(8,128)(2,1)} %bitcast.7), custom_call_target="tpu_custom_call" | custom-call | flops 1073741824 | bytes 25165824 | tf_op jit(solution)/shard_map/gradient_sum/pallas_call | solution.py:389
  270.8 0.1 pad_maximum_fusion.coef_ref
  270.9 78.6 %update_forward.1 = (f32[6,512,2048]{2,1,0:T(8,128)}, f32[6,512,2048]{2,1,0:T(8,128)}, f32[6,2048,512]{2,1,0:T(8,128)}, f32[6,2048,512]{2,1,0:T(8,128)}, bf16[392,512]{1,0:T(8,128)(2,1)S(1)}) custom-call(f32[2]{0:T(128)S(1)} %pad_maximum_fusion.coef_ref, bf16[392,512]{1,0:T(8,128)(2,1)S(1)} %reshape.39.x0_ref, f32[6,512,2048]{2,1,0:T(8,128)} %w1_ref.5, ...), custom_call_target="tpu_custom_call" | custom-call | flops 9865003008 | bytes 226492416 | tf_op jit(solution)/shard_map/update_forward/pallas_call | solution.py:213
  349.4 1.0 reshape.45
  350.4 1.2 reduce_sum.29
  351.6 0.0 all-reduce.2.cloned.1.call-done
  351.6 3.6 multiply_subtract_fusion
  355.2 1.3 fusion
  356.5 0.0 copy-done.1
  (9 shorter events, 0.1 us)
Async XLA Ops:
  7.2 344.5 %all-reduce.2.cloned.1.call-start = ((), (), s32[]{:S(2)}) async-start(), calls=%async_computation | async-start | bytes 2048000 | tf_op jit(solution)/shard_map/psum | solution.py:443
  54.6 1.3 copy-start.3
  54.6 3.0 copy-start
  60.1 5.4 %copy-start.2 = (bf16[2,196,512]{2,0,1:T(2,128)(2,1)S(1)}, bf16[2,196,512]{2,0,1:T(2,128)(2,1)}, u32[]{:S(2)}) copy-start(bf16[2,196,512]{2,0,1:T(2,128)(2,1)} %param.13) | copy-start | bytes 1204228
  355.2 1.3 copy-start.1
Sparse Core Ops, SparseCore 0:
  60.0 153.3 all-reduce.1

commit v2 on v1

v2 whole, which is shorter than its diff:
```python
import functools

import jax
import jax.numpy as jnp
from jax import lax
from jax.experimental import pallas as pl
from jax.experimental.pallas import tpu as pltpu
from jax.sharding import PartitionSpec as P

LN_EPS = 1e-6
GELU_A = 0.7978845608028654
GELU_B = 0.044715
CHUNK = 512
UPD_CHUNK = 1024
FWD_CHUNK = 1024
RING = 4
LANES = 256
MESH_ID = pl.DeviceIdType.MESH
F32 = jnp.float32
BF16 = jnp.bfloat16


def norm_parts(x_f32):
    row_mean = jnp.mean(x_f32, axis=-1, keepdims=True)
    centered = x_f32 - row_mean
    row_var = jnp.mean(centered * centered, axis=-1, keepdims=True)
    inv = lax.rsqrt(row_var + LN_EPS)
    return centered * inv, inv


def gelu_tanh(pre):
    square = pre * pre
    half = 0.5 + 0.5 * jnp.tanh(pre * (GELU_A + (GELU_A * GELU_B) * square))
    return pre * half, half, square


def mm(a, b, dims=((1,), (0,))):
    return lax.dot_general(a, b, (dims, ((), ())), preferred_element_type=F32)


def image_sums(tok_act, images):
    rows = tok_act.shape[0]
    seq = rows // images
    start = lax.broadcasted_iota(jnp.int32, (16, rows), 0) * seq
    row = lax.broadcasted_iota(jnp.int32, (16, rows), 1)
    pick = ((row >= start) & (row < start + seq)).astype(F32).astype(BF16)
    return mm(pick, tok_act)


def cost(flops, bytes_accessed):
    return pl.CostEstimate(flops=flops, bytes_accessed=bytes_accessed, transcendentals=0)


def fwd_body(n_chunk, images, x0_ref, w1_ref, w2_ref, xs_ref, pre_ref, y_ref, x_s, n_s, acc_s):
    layer, step = pl.program_id(0), pl.program_id(1)

    @pl.when((layer == 0) & (step == 0))
    def _():
        x_s[...] = x0_ref[...]

    @pl.when(step == 0)
    def _():
        x_f32 = x_s[...].astype(F32)
        n_s[...] = norm_parts(x_f32)[0].astype(BF16)
        acc_s[...] = x_f32
        xs_ref[0] = x_s[...]

    pre = mm(n_s[...], w1_ref[0].astype(BF16))
    pre_ref[0] = pre
    hidden = gelu_tanh(pre)[0].astype(BF16)
    acc_s[...] += mm(hidden, w2_ref[0].astype(BF16))

    @pl.when(step == n_chunk - 1)
    def _():
        out = acc_s[...].astype(BF16)
        x_s[...] = out
        y_ref[...] = image_sums(out, images)


def forward(x0, images, w_in, w_out):
    layers, d, ff = w_in.shape
    rows = x0.shape[0]
    n_chunk = ff // FWD_CHUNK
    return pl.pallas_call(
        functools.partial(fwd_body, n_chunk, images),
        grid=(layers, n_chunk),
        in_specs=[
            pl.BlockSpec((rows, d), lambda l, j: (0, 0)),
            pl.BlockSpec((1, d, FWD_CHUNK), lambda l, j: (l, 0, j)),
            pl.BlockSpec((1, FWD_CHUNK, d), lambda l, j: (l, j, 0)),
        ],
        out_specs=[
            pl.BlockSpec((1, rows, d), lambda l, j: (l, 0, 0)),
            pl.BlockSpec((1, rows, FWD_CHUNK), lambda l, j: (l, 0, j)),
            pl.BlockSpec((16, d), lambda l, j: (0, 0)),
        ],
        out_shape=[
            jax.ShapeDtypeStruct((layers, rows, d), BF16),
            jax.ShapeDtypeStruct((layers, rows, ff), F32),
            jax.ShapeDtypeStruct((16, d), F32),
        ],
        scratch_shapes=[pltpu.VMEM((rows, d), BF16), pltpu.VMEM((rows, d), BF16), pltpu.VMEM((rows, d), F32)],
        cost_estimate=cost(4 * layers * rows * d * ff, 8 * layers * d * ff + 4 * layers * rows * ff),
        compiler_params=pltpu.CompilerParams(vmem_limit_bytes=48 << 20),
        name="mlp_forward",
    )(x0, w_in, w_out)


def bwd_body(n_chunk, images, dtop_ref, xs_ref, pre_ref, w1_ref, w2_ref, g1_ref, g2_ref, d_s, db_s, n_s, dn_s):
    layer, step = pl.program_id(0), pl.program_id(1)

    @pl.when((layer == 0) & (step == 0))
    def _():
        rows = d_s.shape[0]
        row = lax.broadcasted_iota(jnp.int32, d_s.shape, 0)
        value = jnp.broadcast_to(dtop_ref[0:1, :], d_s.shape)
        for image in range(1, images):
            value = jnp.where(row >= image * (rows // images), dtop_ref[image:image + 1, :], value)
        d_s[...] = value

    @pl.when(step == 0)
    def _():
        db_s[...] = d_s[...].astype(BF16)
        n_s[...] = norm_parts(xs_ref[0].astype(F32))[0].astype(BF16)
        dn_s[...] = jnp.zeros_like(dn_s)

    pre = pre_ref[0]
    gelu, half, square = gelu_tanh(pre)
    hidden = gelu.astype(BF16)
    slope = half + (pre * half) * ((1.0 - half) * (2.0 * GELU_A + (6.0 * GELU_A * GELU_B) * square))
    d_b = db_s[...]
    d_hidden = mm(d_b, w2_ref[0].astype(BF16), ((1,), (1,)))
    d_pre = (slope * d_hidden).astype(BF16)
    g_two = mm(hidden, d_b, ((0,), (0,))).astype(BF16)
    g_one = mm(n_s[...], d_pre, ((0,), (0,))).astype(BF16)
    for part in range(2):
        g1_ref[0, part] = g_one[:, part * LANES:(part + 1) * LANES]
        g2_ref[0, part, 0] = g_two[:, part * LANES:(part + 1) * LANES]
    dn_s[...] += mm(d_pre, w1_ref[0].astype(BF16), ((1,), (1,)))

    @pl.when(step == n_chunk - 1)
    def _():
        normed, inv = norm_parts(xs_ref[0].astype(F32))
        dn = dn_s[...]
        along = jnp.mean(dn * normed, axis=-1, keepdims=True)
        out = d_s[...] + inv * (dn - jnp.mean(dn, axis=-1, keepdims=True) - normed * along)
        d_s[...] = out


def backward(d_top, images, xs, pre, w_in, w_out, first, count):
    _, d, ff = w_in.shape
    rows = xs.shape[1]
    n_chunk = ff // CHUNK
    return pl.pallas_call(
        functools.partial(bwd_body, n_chunk, images),
        grid=(count, n_chunk),
        in_specs=[
            pl.BlockSpec(d_top.shape, lambda l, j: (0, 0)),
            pl.BlockSpec((1, rows, d), lambda l, j: (first - l, 0, 0)),
            pl.BlockSpec((1, rows, CHUNK), lambda l, j: (first - l, 0, j)),
            pl.BlockSpec((1, d, CHUNK), lambda l, j: (first - l, 0, j)),
            pl.BlockSpec((1, CHUNK, d), lambda l, j: (first - l, j, 0)),
        ],
        out_specs=[
            pl.BlockSpec((1, 2, d, LANES), lambda l, j: (first - l, j, 0, 0)),
            pl.BlockSpec((1, 2, 1, CHUNK, LANES), lambda l, j: (first - l, 0, j, 0, 0)),
        ],
        out_shape=[
            jax.ShapeDtypeStruct((count, 2 * n_chunk, d, LANES), BF16),
            jax.ShapeDtypeStruct((count, 2, n_chunk, CHUNK, LANES), BF16),
        ],
        scratch_shapes=[
            pltpu.VMEM((rows, d), F32),
            pltpu.VMEM((rows, d), BF16),
            pltpu.VMEM((rows, d), BF16),
            pltpu.VMEM((rows, d), F32),
        ],
        cost_estimate=cost(8 * count * rows * d * ff, count * (12 * d * ff + 4 * rows * ff)),
        compiler_params=pltpu.CompilerParams(vmem_limit_bytes=56 << 20),
        name="mlp_backward",
    )(d_top, xs, pre, w_in, w_out)


def next_body(n_chunk, images, coef_ref, x0_ref, w1_ref, m1_ref, g1_ref, w2_ref, m2_ref, g2_ref,
              nw1_ref, nm1_ref, nw2_ref, nm2_ref, y_ref, x_s, n_s, acc_s):
    layer, step = pl.program_id(0), pl.program_id(1)
    rate, momentum = coef_ref[0], coef_ref[1]

    @pl.when((layer == 0) & (step == 0))
    def _():
        x_s[...] = x0_ref[...]

    @pl.when(step == 0)
    def _():
        x_f32 = x_s[...].astype(F32)
        n_s[...] = norm_parts(x_f32)[0].astype(BF16)
        acc_s[...] = x_f32

    g_one = jnp.concatenate([g1_ref[0, 0], g1_ref[0, 1], g1_ref[0, 2], g1_ref[0, 3]], axis=1)
    g_two = jnp.concatenate([jnp.concatenate([g2_ref[0, 0, r], g2_ref[0, 1, r]], axis=1) for r in range(2)], axis=0)
    m1 = momentum * m1_ref[0] + g_one.astype(F32)
    w1 = w1_ref[0] - rate * m1
    nm1_ref[0] = m1
    nw1_ref[0] = w1
    m2 = momentum * m2_ref[0] + g_two.astype(F32)
    w2 = w2_ref[0] - rate * m2
    nm2_ref[0] = m2
    nw2_ref[0] = w2
    pre = mm(n_s[...], w1.astype(BF16))
    hidden = gelu_tanh(pre)[0].astype(BF16)
    acc_s[...] += mm(hidden, w2.astype(BF16))

    @pl.when(step == n_chunk - 1)
    def _():
        out = acc_s[...].astype(BF16)
        x_s[...] = out
        y_ref[...] = image_sums(out, images)


def update_forward(coef, x0, images, w_in, mom_in, g_in, w_out, mom_out, g_out):
    layers, d, ff = w_in.shape
    rows = x0.shape[0]
    n_chunk = ff // UPD_CHUNK
    in_block = pl.BlockSpec((1, d, UPD_CHUNK), lambda l, j: (l, 0, j))
    out_block = pl.BlockSpec((1, UPD_CHUNK, d), lambda l, j: (l, j, 0))
    return pl.pallas_call(
        functools.partial(next_body, n_chunk, images),
        grid=(layers, n_chunk),
        in_specs=[
            pl.BlockSpec(memory_space=pltpu.SMEM),
            pl.BlockSpec((rows, d), lambda l, j: (0, 0)),
            in_block,
            in_block,
            pl.BlockSpec((1, 4, d, LANES), lambda l, j: (l, j, 0, 0)),
            out_block,
            out_block,
            pl.BlockSpec((1, 2, 2, 512, LANES), lambda l, j: (l, 0, j, 0, 0)),
        ],
        out_specs=[in_block, in_block, out_block, out_block, pl.BlockSpec((16, d), lambda l, j: (0, 0))],
        out_shape=[
            jax.ShapeDtypeStruct(w_in.shape, F32),
            jax.ShapeDtypeStruct(w_in.shape, F32),
            jax.ShapeDtypeStruct(w_out.shape, F32),
            jax.ShapeDtypeStruct(w_out.shape, F32),
            jax.ShapeDtypeStruct((16, d), F32),
        ],
        scratch_shapes=[pltpu.VMEM((rows, d), BF16), pltpu.VMEM((rows, d), BF16), pltpu.VMEM((rows, d), F32)],
        cost_estimate=cost(4 * layers * rows * d * ff, 36 * layers * d * ff),
        compiler_params=pltpu.CompilerParams(vmem_limit_bytes=60 << 20),
        name="update_forward",
    )(coef, x0, w_in, mom_in, g_in, w_out, mom_out, g_out)


def sum_body(layers, g1_ref, g2_ref, head_ref, o1_ref, o2_ref, all_ref, work, land0, land1, land2, land3, turn, head,
             load_sem, d0_send, d0_recv, ring_send, ring_recv, d1_send, d1_recv, out_sem, head_send, head_recv, head_sem):
    n = RING
    rows = work.shape[2]
    sub = (rows, rows // n, rows // (n * n))
    me = lax.axis_index('data')
    core = lax.rem(me, 2)
    partner = me + 1 - 2 * core
    own, other = core * n, (1 - core) * n
    strides = (2, 2 * n, 2 * n * n)
    pos = [lax.rem(lax.div(me, stride), n) for stride in strides]
    near = [me + (1 - 2 * lax.rem(p, 2)) * stride for p, stride in zip(pos, strides)]
    far = [me + (3 - 2 * p) * stride for p, stride in zip(pos, strides)]
    near_bit = [lax.rem(lax.div(p + 1, 2), 2) for p in pos]
    far_bit = [lax.div(p, 2) for p in pos]

    barrier = pltpu.get_barrier_semaphore()
    greeted = [partner] + near + far
    for device in greeted:
        pl.semaphore_signal(barrier, inc=1, device_id=(device,), device_id_type=MESH_ID)
    pl.semaphore_wait(barrier, len(greeted))

    def each(fn):
        @pl.loop(0, layers // 3)
        def _(i):
            for colour in range(3):
                for kind in range(2):
                    flip = lax.rem(i + kind, 2)
                    layer = colour + 3 * i
                    fn((g1_ref, g2_ref)[kind], (o1_ref, o2_ref)[kind], kind * layers + layer, layer, colour, flip)

    def remote(src, dst, send, recv, device):
        return pltpu.make_async_remote_copy(src_ref=src, dst_ref=dst, send_sem=send, recv_sem=recv, device_id=(device,), device_id_type=MESH_ID)

    def mix(a, b, flip):
        return a + flip * (b - a)

    def bits(colour, flip, stage):
        axis = (colour + stage - 1) % 3
        return mix(near_bit[axis], far_bit[axis], flip), mix(far_bit[axis], near_bit[axis], flip)

    def unit(colour, flip, stage):
        hi, lo = bits(colour, flip, stage)
        return 2 * hi + lo

    def units(m, colour, flip, stage, first, count):
        if stage == 1:
            return work.at[m, pl.ds(own + first, count)]
        row = first * sub[stage - 1]
        if stage == 3:
            row = row + unit(colour, flip, 2) * sub[1]
        row = pl.multiple_of(row, sub[stage - 1])
        return work.at[m, pl.ds(own + unit(colour, flip, 1), 1), pl.ds(row, count * sub[stage - 1])]

    def land(m, stage, step):
        first, count = ((0, 2), (2, 1))[step]
        if stage == 1:
            return land1.at[m, pl.ds(first, count)]
        size = sub[stage - 1]
        return (land2, land3)[stage - 2].at[pl.ds(m, 1), pl.ds(first * size, count * size)]

    def land_unit(m, which):
        return land3.at[pl.ds(m, 1), pl.ds(pl.multiple_of(which * sub[2], sub[2]), sub[2])]

    def copies(t, m, colour, flip):
        scatter = t < 6
        stage = t // 2 + 1 if scatter else 6 - t // 2
        step = t % 2
        hi, lo = bits(colour, flip, stage)
        axis = (colour + stage - 1) % 3
        with_first = (step == 0) == scatter
        to = mix(near[axis], far[axis], flip) if with_first else mix(far[axis], near[axis], flip)
        kept = (2 * hi, 2) if with_first else (2 * hi + lo, 1)
        given = (2 - 2 * hi, 2) if with_first else (2 * hi + 1 - lo, 1)
        if scatter:
            src = turn.at[pl.ds(m, 1)] if t == 5 else units(m, colour, flip, stage, *given)
            return src, land(m, stage, step), land(m, stage, step), to, kept
        src = units(m, colour, flip, stage, *kept)
        return src, src, units(m, colour, flip, stage, *given), to, given

    def message(t, m, colour, flip):
        src, dst, _, to, _ = copies(t, m, colour, flip)
        return remote(src, dst, ring_send.at[m], ring_recv.at[m, t], to)

    def arrival(t, m, colour, flip):
        _, _, here, to, _ = copies(t, m, colour, flip)
        return remote(here, here, ring_send.at[m], ring_recv.at[m, t], to)

    def pair(colour, flip, k):
        hi, _ = bits(colour, flip, 1)
        return mix(2 - 2 * hi, 2 * hi, k)

    def load_copy(g_ref, m, layer, colour, flip, k):
        blocks = pl.ds(own + pair(colour, flip, k), 2)
        return pltpu.make_async_copy(g_ref.at[layer, blocks], work.at[m, blocks], load_sem.at[m, k])

    def swap_copy(g_ref, m, layer, colour, flip, k):
        first = pair(colour, flip, k)
        return remote(g_ref.at[layer, pl.ds(other + first, 2)], land0.at[m, pl.ds(first, 2)], d0_send.at[m, k], d0_recv.at[m, k], partner)

    def final(colour, flip, k):
        hi, lo = bits(colour, flip, 1)
        return ((2 * hi + lo, 1), (2 * hi + 1 - lo, 1), (2 - 2 * hi, 2))[k]

    def share_copy(m, colour, flip, k, half):
        first, count = final(colour, flip, k)
        blocks = work.at[m, pl.ds(half + first, count)]
        return remote(blocks, blocks, d1_send.at[m, k], d1_recv.at[m, k], partner)

    def out_copy(o_ref, m, layer, colour, flip, k, half, slot):
        first, count = final(colour, flip, k)
        blocks = pl.ds(half + first, count)
        return pltpu.make_async_copy(work.at[m, blocks], o_ref.at[layer, blocks], out_sem.at[m, slot])

    def accumulate(dst, sources):
        blocks, count, _ = dst.shape
        step = min(count, 64)

        @pl.loop(0, count // step)
        def _(r):
            part = pl.ds(pl.multiple_of(r * step, step), step)
            for block in range(blocks):
                total = sources[0][block, part, :].astype(F32)
                for source in sources[1:]:
                    total = total + source[block, part, :].astype(F32)
                dst[block, part, :] = total.astype(BF16)

    head_way = 1 - 2 * core

    def head_message(j, back):
        axis, s = divmod(j, n - 1)
        index = lax.rem(pos[axis] - head_way * (s + back) + 2 * n, n)
        to = me + (lax.rem(pos[axis] + head_way + n, n) - pos[axis]) * strides[axis]
        if axis == 0:
            part = head.at[core, pos[2], pos[1], index]
        elif axis == 1:
            part = head.at[core, pos[2], index]
        else:
            part = head.at[core, index]
        return remote(part, part, head_send, head_recv.at[j], to)

    def head_share(which):
        return remote(head.at[which], head.at[which], head_send, head_recv.at[3 * (n - 1)], partner)

    def head_tick(t):
        count = 3 * (n - 1)
        if t == 0:
            first = pltpu.make_async_copy(head_ref, head.at[core, pos[2], pos[1], pos[0]], head_sem)
            first.start()
            first.wait()
        elif t <= count:
            head_message(t - 1, 1).wait_recv()
            head_message(t - 1, 0).wait_send()
        if t < count:
            head_message(t, 0).start()
        elif t == count:
            head_share(core).start()

    for k in range(2):
        def begin(g_ref, o_ref, m, layer, colour, flip, k=k):
            swap_copy(g_ref, m, layer, colour, flip, k).start()
            load_copy(g_ref, m, layer, colour, flip, k).start()
        each(begin)

    for t in range(13):
        def tick(g_ref, o_ref, m, layer, colour, flip, t=t):
            if t > 0:
                arrival(t - 1, m, colour, flip).wait_recv()
                message(t - 1, m, colour, flip).wait_send()
            if t < 2:
                load_copy(g_ref, m, layer, colour, flip, t).wait()
                swap_copy(g_ref, m, layer, colour, flip, t).wait_recv()
                blocks = units(m, colour, flip, 1, pair(colour, flip, t), 2)
                sources = [land0.at[m, pl.ds(pair(colour, flip, t), 2)]] + ([land(m, 1, 0)] if t > 0 else [])
                accumulate(blocks, [blocks] + sources)
            elif t == 5:
                hi, lo = bits(colour, flip, 3)
                mine, theirs = units(m, colour, flip, 3, 2 * hi + lo, 1), units(m, colour, flip, 3, 2 * hi + 1 - lo, 1)
                accumulate(turn.at[pl.ds(m, 1)], [theirs, land_unit(m, 1 - lo)])
                accumulate(mine, [mine, land_unit(m, lo)])
            elif t < 7:
                _, _, here, _, kept = copies(t - 1, m, colour, flip)
                blocks = units(m, colour, flip, (t + 1) // 2, *kept)
                accumulate(blocks, [blocks, here])
            if t < 12:
                message(t, m, colour, flip).start()
            k = t - 10
            if k >= 0:
                share_copy(m, colour, flip, k, own).start()
                out_copy(o_ref, m, layer, colour, flip, k, own, k).start()
            if k >= 1:
                share_copy(m, colour, flip, k - 1, other).wait_recv()
                out_copy(o_ref, m, layer, colour, flip, k - 1, other, k + 2).start()
        each(tick)
        head_tick(t)

    head_share(1 - core).wait_recv()
    head_share(core).wait_send()
    head_out = pltpu.make_async_copy(head, all_ref, head_sem)
    head_out.start()

    def finish(g_ref, o_ref, m, layer, colour, flip):
        share_copy(m, colour, flip, 2, other).wait_recv()
        out_copy(o_ref, m, layer, colour, flip, 2, other, 5).start()
    each(finish)

    def drain(g_ref, o_ref, m, layer, colour, flip):
        for k in range(3):
            share_copy(m, colour, flip, k, own).wait_send()
            out_copy(o_ref, m, layer, colour, flip, k, own, k).wait()
            out_copy(o_ref, m, layer, colour, flip, k, other, k + 3).wait()
        for k in range(2):
            swap_copy(g_ref, m, layer, colour, flip, k).wait_send()
    each(drain)
    head_out.wait()


def sum_gradients(g1, g2, head_part, group_size):
    n = RING
    if group_size != 2 * n ** 3:
        raise ValueError("needs a 4x4x4 torus")
    layers, blocks, rows, lanes = g1.shape
    count = 2 * layers
    dma = pltpu.SemaphoreType.DMA
    head_shape = (2, n, n, n) + head_part.shape
    return pl.pallas_call(
        functools.partial(sum_body, layers),
        in_specs=[pl.BlockSpec(memory_space=pl.ANY)] * 3,
        out_specs=[pl.BlockSpec(memory_space=pl.ANY)] * 3,
        out_shape=[
            jax.ShapeDtypeStruct(g1.shape, BF16),
            jax.ShapeDtypeStruct(g2.shape, BF16),
            jax.ShapeDtypeStruct(head_shape, BF16),
        ],
        scratch_shapes=[
            pltpu.VMEM((count, blocks, rows, lanes), BF16),
            pltpu.VMEM((count, n, rows, lanes), BF16),
            pltpu.VMEM((count, 3, rows, lanes), BF16),
            pltpu.VMEM((count, 3 * rows // n, lanes), BF16),
            pltpu.VMEM((count, 3 * rows // (n * n), lanes), BF16),
            pltpu.VMEM((count, rows // (n * n), lanes), BF16),
            pltpu.VMEM(head_shape, BF16),
            dma((count, 2)),
            dma((count, 2)),
            dma((count, 2)),
            dma((count,)),
            dma((count, 12)),
            dma((count, 3)),
            dma((count, 3)),
            dma((count, 6)),
            dma,
            dma((3 * (n - 1) + 1,)),
            dma,
        ],
        cost_estimate=cost(1 << 30, 4 * g1.size),
        compiler_params=pltpu.CompilerParams(collective_id=0, has_side_effects=True, vmem_limit_bytes=60 << 20),
        name="gradient_sum",
    )(g1, g2, head_part)


def head_backward(pooled, lab_row, w_head_b, examples):
    logits = jnp.dot(pooled, w_head_b, preferred_element_type=F32)
    soft_prob = jax.nn.softmax(logits, axis=-1)
    onehot = (lab_row[:, None] == jnp.arange(logits.shape[1])[None, :]).astype(F32)
    d_logits = ((soft_prob - onehot) / examples).astype(BF16)
    d_pooled = jnp.einsum('bc,dc->bd', d_logits, w_head_b, preferred_element_type=F32)
    return d_logits, d_pooled


def solution(mesh):
    group_size = mesh.shape['data']

    def local_step(x_step, labels, x_next, w_in, w_out, w_head, mom_in, mom_out, mom_head, learn_rate, mom_coef):
        micro_count, images, seq, d = x_step.shape
        layers = w_in.shape[0]
        classes = w_head.shape[1]
        batch = micro_count * images
        examples = batch * group_size
        xs, pre, sums = forward(x_step.reshape(-1, d), batch, w_in, w_out)
        pooled = (sums[:batch] / seq).astype(BF16)
        d_logits, d_pooled = head_backward(pooled, labels.reshape(-1), w_head.astype(BF16), examples)
        wide = -(-classes // 512) * 512
        head_part = jnp.concatenate([pooled, jnp.pad(d_logits, ((0, 0), (0, wide - classes)))], axis=1)
        d_top = jnp.pad(d_pooled / seq, ((0, 8 - batch), (0, 0)))
        g_in, g_out = backward(d_top, batch, xs, pre, w_in, w_out, layers - 1, layers)
        block_shape = (layers, -1) + g_out.shape[3:]
        red_in, red_out, head_all = sum_gradients(g_in, g_out.reshape(block_shape), head_part.reshape(16, -1), group_size)
        coef = jnp.stack([learn_rate, mom_coef])
        new_w_in, new_mom_in, new_w_out, new_mom_out, next_sums = update_forward(coef, x_next.reshape(-1, d), images, w_in, mom_in, red_in, w_out, mom_out, red_out.reshape(g_out.shape))
        head_rows = head_all.reshape(examples, d + wide)
        g_head = jnp.einsum('bd,bc->dc', head_rows[:, :d], head_rows[:, d:d + classes], preferred_element_type=F32)
        new_mom_head = mom_coef * mom_head + g_head
        new_w_head = w_head - learn_rate * new_mom_head
        next_pooled = (next_sums[:images] / seq).astype(BF16)
        logits_next = jnp.dot(next_pooled, new_w_head.astype(BF16), preferred_element_type=F32)
        return (logits_next, new_w_in, new_w_out, new_w_head, new_mom_in, new_mom_out, new_mom_head)

    return jax.shard_map(local_step, mesh=mesh, in_specs=(P(None, 'data', None, None), P(None, 'data'), P('data', None, None), P(), P(), P(), P(), P(), P(), P(), P()), out_specs=(P('data', None), P(), P(), P(), P(), P(), P()), check_vma=False)
```

time: 365 us -> 334 us (0.915)
  Pallas kernels: 330 us -> 315 us
  between operations: 15.4 us -> 2 us
  other arithmetic: 6.65 us -> 0.89 us
    pallas_call x4, Pallas kernels: 330 us -> 315 us  [the longest x1 127 us: sum_gradients(): pl.pallas_call(functools.partial(sum_body, layers), in_specs=[pl.BlockSpe...]
  transfers between devices with their start and end apart: 1 -> 0, of which waited for: 0 -> 0; matrix products, arithmetic and copies ran while one was open for 2% -> 0% of each run, Pallas kernels for 78% -> 0%
where the time goes in v2:
time: 334 us
  Pallas kernels  315 us (94%)
  local copies, waits for them, and re-layouts  9.53 us (3%)
  matrix products  6.21 us (2%)
    pallas_call x1, Pallas kernels, sum_gradients(): pl.pallas_call(functools.partial(sum_body, layers), in_specs=[pl.BlockSpe...  127 us
    pallas_call x1, Pallas kernels, backward(): pl.pallas_call(functools.partial(bwd_body, n_chunk, images), grid=(count,...  76.6 us
    pallas_call x1, Pallas kernels, update_forward(): pl.pallas_call(functools.partial(next_body, n_chunk, images), grid=(layer...  70.8 us
    pallas_call x1, Pallas kernels, forward(): pl.pallas_call(functools.partial(fwd_body, n_chunk, images), grid=(layers...  40.9 us

profile of v2, /device:TPU:1, one launch (start us, length us, event | category | flops | bytes accessed | tf_op | source)
XLA Modules:
  0.0 333.9 jit_solution(5278955913511937487)
XLA Ops:
  0.6 1.2 copy.21
  1.9 0.1 reshape.36.x0_ref
  2.0 0.0 copy-start.1
  2.0 40.9 %mlp_forward.1 = (bf16[6,784,512]{2,1,0:T(8,128)(2,1)S(1)}, f32[6,784,2048]{2,1,0:T(8,128)}, f32[16,512]{1,0:T(8,128)S(1)}) custom-call(bf16[784,512]{1,0:T(8,128)(2,1)S(1)} %reshape.36.x0_ref, f32[6,512,2048]{2,1,0:T(8,128)} %w1_ref.5, f32[6,2048,512]{2,1,0:T(8,128)} %w2_ref.5), custom_call_target="tpu_custom_call" | custom-call | flops 19730006016 | bytes 88866816 | tf_op jit(solution)/shard_map/mlp_forward/pallas_call | solution.py:84
  43.0 2.2 copy-done
  45.2 0.0 copy-done.1
  45.2 0.5 fusion.12
  45.7 0.2 fusion.8
  45.9 0.0 copy-done.5
  45.9 0.1 eq.15
  46.0 0.1 multiply_convert_fusion
  46.1 0.3 convolution_multiply_fusion
  46.4 0.6 pad.8.dtop_ref
  47.0 76.6 %mlp_backward.1 = (bf16[6,8,512,256]{3,2,1,0:T(8,128)(2,1)}, bf16[6,2,4,512,256]{4,3,2,1,0:T(8,128)(2,1)}) custom-call(f32[8,512]{1,0:T(8,128)} %pad.8.dtop_ref, bf16[6,784,512]{2,1,0:T(8,128)(2,1)} %copy-done, f32[6,784,2048]{2,1,0:T(8,128)} %get-tuple-element.22.pre_ref, f32[6,512,2048]{2,1,0:T(8,128)} %w1_ref.5, f32[6,2048,512]{2,1,0:T(8,128)} %w2_ref.5), custom_call_target="tpu_custom_call" | custom-call | flops 39460012032 | bytes 114032640 | tf_op jit(solution)/shard_map/mlp_backward/pallas_call | solution.py:154
  123.6 0.6 reshape.38.head_ref
  124.2 126.9 %gradient_sum.1 = (bf16[6,8,512,256]{3,2,1,0:T(8,128)(2,1)}, bf16[6,8,512,256]{3,2,1,0:T(8,128)(2,1)}, bf16[2,4,4,4,16,384]{5,4,3,2,1,0:T(8,128)(2,1)}) custom-call(bf16[6,8,512,256]{3,2,1,0:T(8,128)(2,1)} %get-tuple-element.23.g1_ref, bf16[6,8,512,256]{3,2,1,0:T(8,128)(2,1)} %bitcast.11, bf16[16,384]{1,0:T(8,128)(2,1)} %reshape.38.head_ref), custom_call_target="tpu_custom_call" | custom-call | flops 1073741824 | bytes 25165824 | tf_op jit(solution)/shard_map/gradient_sum/pallas_call | solution.py:479
  252.4 0.6 pad_maximum_fusion.coef_ref
  253.0 0.0 copy-done.3
  253.0 0.8 reshape.35.x0_ref
  253.9 70.8 %update_forward.1 = (f32[6,512,2048]{2,1,0:T(8,128)}, f32[6,512,2048]{2,1,0:T(8,128)}, f32[6,2048,512]{2,1,0:T(8,128)}, f32[6,2048,512]{2,1,0:T(8,128)}, f32[16,512]{1,0:T(8,128)}) custom-call(f32[2]{0:T(128)} %pad_maximum_fusion.coef_ref, bf16[392,512]{1,0:T(8,128)(2,1)} %reshape.35.x0_ref, f32[6,512,2048]{2,1,0:T(8,128)} %w1_ref.5, ...), custom_call_target="tpu_custom_call" | custom-call | flops 9865003008 | bytes 226492416 | tf_op jit(solution)/shard_map/update_forward/pallas_call | solution.py:226
  324.7 3.7 %reshape.40 = bf16[512,1536]{1,0:T(8,128)(2,1)} reshape(bf16[2,4,4,4,16,384]{5,4,3,2,1,0:T(8,128)(2,1)} %get-tuple-element.28) | data formatting | bytes 3145728 | tf_op jit(solution)/shard_map/reshape | solution.py:543
  328.4 4.2 %multiply_subtract_fusion = (f32[512,1000]{0,1:T(8,128)S(1)}, f32[512,1000]{0,1:T(8,128)}) fusion(f32[512,1000]{0,1:T(8,128)S(1)} %copy-done.1, f32[]{:T(128)} %copy.22, bf16[512,1536]{1,0:T(8,128)(2,1)} %reshape.40, f32[512,1000]{0,1:T(8,128)} %param.19, f32[]{:T(128)} %copy.23), kind=kOutput, calls=%fused_computation | convolution fusion | flops 526336000 | bytes 9764872 | tf_op jit(solution)/shard_map/bd,bc->dc/dot_general | solution.py:544
  332.6 1.3 fusion.1
  333.8 0.0 copy-done.2
  (9 shorter events, 0.1 us)
Async XLA Ops:
  2.0 43.2 %copy-start.1 = (f32[512,1000]{0,1:T(8,128)S(1)}, f32[512,1000]{0,1:T(8,128)}, u32[]{:S(2)}) copy-start(f32[512,1000]{0,1:T(8,128)} %param.16) | copy-start | bytes 6144004
  43.0 2.2 copy-start
  45.2 0.7 copy-start.5
  124.2 128.8 %copy-start.3 = (bf16[2,196,512]{2,0,1:T(2,128)(2,1)S(1)}, bf16[2,196,512]{2,0,1:T(2,128)(2,1)}, u32[]{:S(2)}) copy-start(bf16[2,196,512]{2,0,1:T(2,128)(2,1)} %param.13) | copy-start | bytes 1204228
  328.4 4.2 %copy-start.4 = (f32[16,512]{1,0:T(8,128)S(1)}, f32[16,512]{1,0:T(8,128)}, u32[]{:S(2)}) copy-start(f32[16,512]{1,0:T(8,128)} %get-tuple-element.27) | copy-start | bytes 98308
  332.6 1.3 copy-start.2

commit v3 on v2

--- a/solution.py
+++ b/solution.py
@@ -106,9 +106,7 @@
     )(x0, w_in, w_out)
 
 
-def bwd_body(n_chunk, images, dtop_ref, xs_ref, pre_ref, w1_ref, w2_ref, g1_ref, g2_ref, d_s, db_s, n_s, dn_s):
-    layer, step = pl.program_id(0), pl.program_id(1)
-
+def backward_step(n_chunk, images, layer, step, slot_wait, slot_send, dtop_ref, xs_ref, pre_ref, w1_ref, w2_ref, g_s, d_s, db_s, n_s, dn_s):
     @pl.when((layer == 0) & (step == 0))
     def _():
         rows = d_s.shape[0]
@@ -133,9 +131,11 @@
     d_pre = (slope * d_hidden).astype(BF16)
     g_two = mm(hidden, d_b, ((0,), (0,))).astype(BF16)
     g_one = mm(n_s[...], d_pre, ((0,), (0,))).astype(BF16)
+    slot = slot_wait()
     for part in range(2):
-        g1_ref[0, part] = g_one[:, part * LANES:(part + 1) * LANES]
-        g2_ref[0, part, 0] = g_two[:, part * LANES:(part + 1) * LANES]
+        g_s[slot, part] = g_one[:, part * LANES:(part + 1) * LANES]
+        g_s[slot, 2 + part] = g_two[:, part * LANES:(part + 1) * LANES]
+    slot_send()
     dn_s[...] += mm(d_pre, w1_ref[0].astype(BF16), ((1,), (1,)))
 
     @pl.when(step == n_chunk - 1)
@@ -145,40 +145,6 @@
         along = jnp.mean(dn * normed, axis=-1, keepdims=True)
         out = d_s[...] + inv * (dn - jnp.mean(dn, axis=-1, keepdims=True) - normed * along)
         d_s[...] = out
-
-
-def backward(d_top, images, xs, pre, w_in, w_out, first, count):
-    _, d, ff = w_in.shape
-    rows = xs.shape[1]
-    n_chunk = ff // CHUNK
-    return pl.pallas_call(
-        functools.partial(bwd_body, n_chunk, images),
-        grid=(count, n_chunk),
-        in_specs=[
-            pl.BlockSpec(d_top.shape, lambda l, j: (0, 0)),
-            pl.BlockSpec((1, rows, d), lambda l, j: (first - l, 0, 0)),
-            pl.BlockSpec((1, rows, CHUNK), lambda l, j: (first - l, 0, j)),
-            pl.BlockSpec((1, d, CHUNK), lambda l, j: (first - l, 0, j)),
-            pl.BlockSpec((1, CHUNK, d), lambda l, j: (first - l, j, 0)),
-        ],
-        out_specs=[
-            pl.BlockSpec((1, 2, d, LANES), lambda l, j: (first - l, j, 0, 0)),
-            pl.BlockSpec((1, 2, 1, CHUNK, LANES), lambda l, j: (first - l, 0, j, 0, 0)),
-        ],
-        out_shape=[
-            jax.ShapeDtypeStruct((count, 2 * n_chunk, d, LANES), BF16),
-            jax.ShapeDtypeStruct((count, 2, n_chunk, CHUNK, LANES), BF16),
-        ],
-        scratch_shapes=[
-            pltpu.VMEM((rows, d), F32),
-            pltpu.VMEM((rows, d), BF16),
-            pltpu.VMEM((rows, d), BF16),
-            pltpu.VMEM((rows, d), F32),
-        ],
-        cost_estimate=cost(8 * count * rows * d * ff, count * (12 * d * ff + 4 * rows * ff)),
-        compiler_params=pltpu.CompilerParams(vmem_limit_bytes=56 << 20),
-        name="mlp_backward",
-    )(d_top, xs, pre, w_in, w_out)
 
 
 def next_body(n_chunk, images, coef_ref, x0_ref, w1_ref, m1_ref, g1_ref, w2_ref, m2_ref, g2_ref,
@@ -251,8 +217,11 @@
     )(coef, x0, w_in, mom_in, g_in, w_out, mom_out, g_out)
 
 
-def sum_body(layers, g1_ref, g2_ref, head_ref, o1_ref, o2_ref, all_ref, work, land0, land1, land2, land3, turn, head,
-             load_sem, d0_send, d0_recv, ring_send, ring_recv, d1_send, d1_recv, out_sem, head_send, head_recv, head_sem):
+def backward_sum_body(layers, n_chunk, images, dtop_ref, xs_ref, pre_ref, w1_ref, w2_ref, head_ref, o1_ref, o2_ref, all_ref, g1_ref, g2_ref,
+                      g_s, d_s, db_s, n_s, dn_s, work, land0, land1, land2, land3, turn, head,
+                      g_sem, load_sem, d0_send, d0_recv, ring_send, ring_recv, d1_send, d1_recv, out_sem, head_send, head_recv, head_sem, credit):
+    layer_index, step_index = pl.program_id(0), pl.program_id(1)
+    grid_step = layer_index * n_chunk + step_index
     n = RING
     rows = work.shape[2]
     sub = (rows, rows // n, rows // (n * n))
@@ -269,18 +238,18 @@
 
     barrier = pltpu.get_barrier_semaphore()
     greeted = [partner] + near + far
-    for device in greeted:
-        pl.semaphore_signal(barrier, inc=1, device_id=(device,), device_id_type=MESH_ID)
-    pl.semaphore_wait(barrier, len(greeted))
-
-    def each(fn):
-        @pl.loop(0, layers // 3)
-        def _(i):
-            for colour in range(3):
-                for kind in range(2):
-                    flip = lax.rem(i + kind, 2)
-                    layer = colour + 3 * i
-                    fn((g1_ref, g2_ref)[kind], (o1_ref, o2_ref)[kind], kind * layers + layer, layer, colour, flip)
+
+    @pl.when(grid_step == 0)
+    def _():
+        for device in greeted:
+            pl.semaphore_signal(barrier, inc=1, device_id=(device,), device_id_type=MESH_ID)
+        pl.semaphore_wait(barrier, len(greeted))
+
+    def each(wave, fn):
+        for colour in range(3):
+            for kind in range(2):
+                layer = colour + 3 * wave
+                fn((g1_ref, g2_ref)[kind], (o1_ref, o2_ref)[kind], kind * layers + layer, layer, colour, (wave + kind) % 2)
 
     def remote(src, dst, send, recv, device):
         return pltpu.make_async_remote_copy(src_ref=src, dst_ref=dst, send_sem=send, recv_sem=recv, device_id=(device,), device_id_type=MESH_ID)
@@ -298,12 +267,12 @@
 
     def units(m, colour, flip, stage, first, count):
         if stage == 1:
-            return work.at[m, pl.ds(own + first, count)]
+            return work.at[m, pl.ds(first, count)]
         row = first * sub[stage - 1]
         if stage == 3:
             row = row + unit(colour, flip, 2) * sub[1]
         row = pl.multiple_of(row, sub[stage - 1])
-        return work.at[m, pl.ds(own + unit(colour, flip, 1), 1), pl.ds(row, count * sub[stage - 1])]
+        return work.at[m, pl.ds(unit(colour, flip, 1), 1), pl.ds(row, count * sub[stage - 1])]
 
     def land(m, stage, step):
         first, count = ((0, 2), (2, 1))[step]
@@ -343,27 +312,28 @@
         hi, _ = bits(colour, flip, 1)
         return mix(2 - 2 * hi, 2 * hi, k)
 
+    def cell(m):
+        return m // layers * 3 + m % 3
+
     def load_copy(g_ref, m, layer, colour, flip, k):
-        blocks = pl.ds(own + pair(colour, flip, k), 2)
-        return pltpu.make_async_copy(g_ref.at[layer, blocks], work.at[m, blocks], load_sem.at[m, k])
+        first = pair(colour, flip, k)
+        return pltpu.make_async_copy(g_ref.at[layer, pl.ds(own + first, 2)], work.at[m, pl.ds(first, 2)], load_sem.at[m, k])
 
     def swap_copy(g_ref, m, layer, colour, flip, k):
         first = pair(colour, flip, k)
-        return remote(g_ref.at[layer, pl.ds(other + first, 2)], land0.at[m, pl.ds(first, 2)], d0_send.at[m, k], d0_recv.at[m, k], partner)
+        return remote(g_ref.at[layer, pl.ds(other + first, 2)], land0.at[cell(m), pl.ds(first, 2)], d0_send.at[m, k], d0_recv.at[m, k], partner)
 
     def final(colour, flip, k):
         hi, lo = bits(colour, flip, 1)
         return ((2 * hi + lo, 1), (2 * hi + 1 - lo, 1), (2 - 2 * hi, 2))[k]
 
-    def share_copy(m, colour, flip, k, half):
+    def share_copy(o_ref, m, layer, colour, flip, k, half):
         first, count = final(colour, flip, k)
-        blocks = work.at[m, pl.ds(half + first, count)]
-        return remote(blocks, blocks, d1_send.at[m, k], d1_recv.at[m, k], partner)
-
-    def out_copy(o_ref, m, layer, colour, flip, k, half, slot):
+        return remote(work.at[m, pl.ds(first, count)], o_ref.at[layer, pl.ds(half + first, count)], d1_send.at[m, k], d1_recv.at[m, k], partner)
+
+    def out_copy(o_ref, m, layer, colour, flip, k):
         first, count = final(colour, flip, k)
-        blocks = pl.ds(half + first, count)
-        return pltpu.make_async_copy(work.at[m, blocks], o_ref.at[layer, blocks], out_sem.at[m, slot])
+        return pltpu.make_async_copy(work.at[m, pl.ds(first, count)], o_ref.at[layer, pl.ds(own + first, count)], out_sem.at[m, k])
 
     def accumulate(dst, sources):
         blocks, count, _ = dst.shape
@@ -409,14 +379,15 @@
         elif t == count:
             head_share(core).start()
 
-    for k in range(2):
-        def begin(g_ref, o_ref, m, layer, colour, flip, k=k):
-            swap_copy(g_ref, m, layer, colour, flip, k).start()
-            load_copy(g_ref, m, layer, colour, flip, k).start()
-        each(begin)
-
-    for t in range(13):
-        def tick(g_ref, o_ref, m, layer, colour, flip, t=t):
+    def begin(wave):
+        for k in range(2):
+            def body(g_ref, o_ref, m, layer, colour, flip, k=k):
+                swap_copy(g_ref, m, layer, colour, flip, k).start()
+                load_copy(g_ref, m, layer, colour, flip, k).start()
+            each(wave, body)
+
+    def tick(wave, t):
+        def body(g_ref, o_ref, m, layer, colour, flip):
             if t > 0:
                 arrival(t - 1, m, colour, flip).wait_recv()
                 message(t - 1, m, colour, flip).wait_send()
@@ -424,7 +395,7 @@
                 load_copy(g_ref, m, layer, colour, flip, t).wait()
                 swap_copy(g_ref, m, layer, colour, flip, t).wait_recv()
                 blocks = units(m, colour, flip, 1, pair(colour, flip, t), 2)
-                sources = [land0.at[m, pl.ds(pair(colour, flip, t), 2)]] + ([land(m, 1, 0)] if t > 0 else [])
+                sources = [land0.at[cell(m), pl.ds(pair(colour, flip, t), 2)]] + ([land(m, 1, 0)] if t > 0 else [])
                 accumulate(blocks, [blocks] + sources)
             elif t == 5:
                 hi, lo = bits(colour, flip, 3)
@@ -439,60 +410,114 @@
                 message(t, m, colour, flip).start()
             k = t - 10
             if k >= 0:
-                share_copy(m, colour, flip, k, own).start()
-                out_copy(o_ref, m, layer, colour, flip, k, own, k).start()
-            if k >= 1:
-                share_copy(m, colour, flip, k - 1, other).wait_recv()
-                out_copy(o_ref, m, layer, colour, flip, k - 1, other, k + 2).start()
-        each(tick)
-        head_tick(t)
-
-    head_share(1 - core).wait_recv()
-    head_share(core).wait_send()
-    head_out = pltpu.make_async_copy(head, all_ref, head_sem)
-    head_out.start()
-
-    def finish(g_ref, o_ref, m, layer, colour, flip):
-        share_copy(m, colour, flip, 2, other).wait_recv()
-        out_copy(o_ref, m, layer, colour, flip, 2, other, 5).start()
-    each(finish)
-
-    def drain(g_ref, o_ref, m, layer, colour, flip):
-        for k in range(3):
-            share_copy(m, colour, flip, k, own).wait_send()
-            out_copy(o_ref, m, layer, colour, flip, k, own, k).wait()
-            out_copy(o_ref, m, layer, colour, flip, k, other, k + 3).wait()
-        for k in range(2):
-            swap_copy(g_ref, m, layer, colour, flip, k).wait_send()
-    each(drain)
-    head_out.wait()
-
-
-def sum_gradients(g1, g2, head_part, group_size):
+                share_copy(o_ref, m, layer, colour, flip, k, own).start()
+                out_copy(o_ref, m, layer, colour, flip, k).start()
+        each(wave, body)
+
+    def finish(wave):
+        def body(g_ref, o_ref, m, layer, colour, flip):
+            for k in range(3):
+                share_copy(o_ref, m, layer, colour, flip, k, own).wait_send()
+                share_copy(o_ref, m, layer, colour, flip, k, other).wait_recv()
+                out_copy(o_ref, m, layer, colour, flip, k).wait()
+            for k in range(2):
+                swap_copy(g_ref, m, layer, colour, flip, k).wait_send()
+        each(wave, body)
+
+    real_layer = layers - 1 - layer_index
+    slot = lax.rem(step_index, 2)
+
+    def slot_copies(which, at_step):
+        blocks = [(g1_ref, 2 * at_step), (g1_ref, 2 * at_step + 1), (g2_ref, at_step), (g2_ref, n_chunk + at_step)]
+        return [pltpu.make_async_copy(g_s.at[which, q], ref.at[real_layer, block], g_sem.at[which, q]) for q, (ref, block) in enumerate(blocks)]
+
+    def slot_wait():
+        @pl.when(step_index >= 2)
+        def _():
+            for copy in slot_copies(slot, step_index - 2):
+                copy.wait()
+        return slot
+
+    def slot_send():
+        for copy in slot_copies(slot, step_index):
+            copy.start()
+
+    backward_step(n_chunk, images, layer_index, step_index, slot_wait, slot_send, dtop_ref, xs_ref, pre_ref, w1_ref, w2_ref, g_s, d_s, db_s, n_s, dn_s)
+
+    @pl.when(step_index == n_chunk - 1)
+    def _():
+        for past in (1, 0):
+            for copy in slot_copies((n_chunk - 1 - past) % 2, n_chunk - 1 - past):
+                copy.wait()
+
+    half_way = layers // 2 * n_chunk
+    plan = {half_way - 1: [lambda: begin(1)]}
+    for offset, t in ((0, 0), (4, 1), (6, 2), (8, 3), (9, 4), (10, 5), (11, 6)):
+        plan.setdefault(half_way + offset, []).append(functools.partial(tick, 1, t))
+    plan[half_way + 4].append(lambda: pl.semaphore_signal(credit, inc=1, device_id=(partner,), device_id_type=MESH_ID))
+    for t in range(3 * (n - 1) + 1):
+        plan.setdefault(half_way + t, []).append(functools.partial(head_tick, t))
+    rest = [lambda: pl.semaphore_wait(credit, 1), lambda: begin(0)]
+    for wave, t in ((1, 7), (1, 8), (0, 0), (1, 9), (0, 1), (1, 10), (0, 2), (0, 3), (1, 11), (0, 4), (0, 5), (0, 6), (0, 7), (1, 12), (0, 8), (0, 9), (0, 10), (0, 11), (0, 12)):
+        rest.append(functools.partial(tick, wave, t))
+    plan[2 * half_way - 1] += rest
+    for when, actions in plan.items():
+        @pl.when(grid_step == when)
+        def _(actions=actions):
+            for action in actions:
+                action()
+
+    @pl.when(grid_step == 2 * half_way - 1)
+    def _():
+        head_share(1 - core).wait_recv()
+        head_share(core).wait_send()
+        head_out = pltpu.make_async_copy(head, all_ref, head_sem)
+        head_out.start()
+        finish(1)
+        finish(0)
+        head_out.wait()
+
+
+def backward_sum(d_top, images, xs, pre, w_in, w_out, head_part, group_size):
     n = RING
     if group_size != 2 * n ** 3:
         raise ValueError("needs a 4x4x4 torus")
-    layers, blocks, rows, lanes = g1.shape
+    layers, d, ff = w_in.shape
+    rows = xs.shape[1]
+    n_chunk = ff // CHUNK
     count = 2 * layers
+    size = CHUNK
     dma = pltpu.SemaphoreType.DMA
     head_shape = (2, n, n, n) + head_part.shape
+    sums = jax.ShapeDtypeStruct((layers, 2 * n, size, LANES), BF16)
+    last = layers - 1
     return pl.pallas_call(
-        functools.partial(sum_body, layers),
-        in_specs=[pl.BlockSpec(memory_space=pl.ANY)] * 3,
-        out_specs=[pl.BlockSpec(memory_space=pl.ANY)] * 3,
-        out_shape=[
-            jax.ShapeDtypeStruct(g1.shape, BF16),
-            jax.ShapeDtypeStruct(g2.shape, BF16),
-            jax.ShapeDtypeStruct(head_shape, BF16),
-        ],
+        functools.partial(backward_sum_body, layers, n_chunk, images),
+        grid=(layers, n_chunk),
+        in_specs=[
+            pl.BlockSpec(d_top.shape, lambda l, j: (0, 0)),
+            pl.BlockSpec((1, rows, d), lambda l, j: (last - l, 0, 0)),
+            pl.BlockSpec((1, rows, CHUNK), lambda l, j: (last - l, 0, j)),
+            pl.BlockSpec((1, d, CHUNK), lambda l, j: (last - l, 0, j)),
+            pl.BlockSpec((1, CHUNK, d), lambda l, j: (last - l, j, 0)),
+            pl.BlockSpec(memory_space=pl.ANY),
+        ],
+        out_specs=[pl.BlockSpec(memory_space=pl.ANY)] * 5,
+        out_shape=[sums, sums, jax.ShapeDtypeStruct(head_shape, BF16), sums, sums],
         scratch_shapes=[
-            pltpu.VMEM((count, blocks, rows, lanes), BF16),
-            pltpu.VMEM((count, n, rows, lanes), BF16),
-            pltpu.VMEM((count, 3, rows, lanes), BF16),
-            pltpu.VMEM((count, 3 * rows // n, lanes), BF16),
-            pltpu.VMEM((count, 3 * rows // (n * n), lanes), BF16),
-            pltpu.VMEM((count, rows // (n * n), lanes), BF16),
+            pltpu.VMEM((2, 4, size, LANES), BF16),
+            pltpu.VMEM((rows, d), F32),
+            pltpu.VMEM((rows, d), BF16),
+            pltpu.VMEM((rows, d), BF16),
+            pltpu.VMEM((rows, d), F32),
+            pltpu.VMEM((count, n, size, LANES), BF16),
+            pltpu.VMEM((6, n, size, LANES), BF16),
+            pltpu.VMEM((count, 3, size, LANES), BF16),
+            pltpu.VMEM((count, 3 * size // n, LANES), BF16),
+            pltpu.VMEM((count, 3 * size // (n * n), LANES), BF16),
+            pltpu.VMEM((count, size // (n * n), LANES), BF16),
             pltpu.VMEM(head_shape, BF16),
+            dma((2, 4)),
             dma((count, 2)),
             dma((count, 2)),
             dma((count, 2)),
@@ -500,15 +525,16 @@
             dma((count, 12)),
             dma((count, 3)),
             dma((count, 3)),
-            dma((count, 6)),
+            dma((count, 3)),
             dma,
             dma((3 * (n - 1) + 1,)),
             dma,
-        ],
-        cost_estimate=cost(1 << 30, 4 * g1.size),
-        compiler_params=pltpu.CompilerParams(collective_id=0, has_side_effects=True, vmem_limit_bytes=60 << 20),
-        name="gradient_sum",
-    )(g1, g2, head_part)
+            pltpu.SemaphoreType.REGULAR,
+        ],
+        cost_estimate=cost(8 * layers * rows * d * ff, layers * (12 * d * ff + 4 * rows * ff)),
+        compiler_params=pltpu.CompilerParams(collective_id=0, has_side_effects=True, vmem_limit_bytes=63 << 20),
+        name="backward_sum",
+    )(d_top, xs, pre, w_in, w_out, head_part)
 
 
 def head_backward(pooled, lab_row, w_head_b, examples):
@@ -535,11 +561,9 @@
         wide = -(-classes // 512) * 512
         head_part = jnp.concatenate([pooled, jnp.pad(d_logits, ((0, 0), (0, wide - classes)))], axis=1)
         d_top = jnp.pad(d_pooled / seq, ((0, 8 - batch), (0, 0)))
-        g_in, g_out = backward(d_top, batch, xs, pre, w_in, w_out, layers - 1, layers)
-        block_shape = (layers, -1) + g_out.shape[3:]
-        red_in, red_out, head_all = sum_gradients(g_in, g_out.reshape(block_shape), head_part.reshape(16, -1), group_size)
+        red_in, red_out, head_all, _, _ = backward_sum(d_top, batch, xs, pre, w_in, w_out, head_part.reshape(16, -1), group_size)
         coef = jnp.stack([learn_rate, mom_coef])
-        new_w_in, new_mom_in, new_w_out, new_mom_out, next_sums = update_forward(coef, x_next.reshape(-1, d), images, w_in, mom_in, red_in, w_out, mom_out, red_out.reshape(g_out.shape))
+        new_w_in, new_mom_in, new_w_out, new_mom_out, next_sums = update_forward(coef, x_next.reshape(-1, d), images, w_in, mom_in, red_in, w_out, mom_out, red_out.reshape(layers, 2, -1, CHUNK, LANES))
         head_rows = head_all.reshape(examples, d + wide)
         g_head = jnp.einsum('bd,bc->dc', head_rows[:, :d], head_rows[:, d:d + classes], preferred_element_type=F32)
         new_mom_head = mom_coef * mom_head + g_head

time: 334 us -> 338 us (1.012)
  Pallas kernels: 315 us -> 319 us
    pallas_call x2 -> x1, Pallas kernels: 203 us -> 208 us  [backward_sum(): pl.pallas_call(functools.partial(backward_sum_body, layers, n_chunk, imag...]
where the time goes in v3:
time: 338 us
  Pallas kernels  319 us (94%)
  local copies, waits for them, and re-layouts  9.67 us (3%)
  matrix products  6.21 us (2%)
    pallas_call x1, Pallas kernels, backward_sum(): pl.pallas_call(functools.partial(backward_sum_body, layers, n_chunk, imag...  208 us
    pallas_call x1, Pallas kernels, update_forward(): pl.pallas_call(functools.partial(next_body, n_chunk, images), grid=(layer...  70.7 us
    pallas_call x1, Pallas kernels, forward(): pl.pallas_call(functools.partial(fwd_body, n_chunk, images), grid=(layers...  40.9 us

profile of v3, /device:TPU:1, one launch (start us, length us, event | category | flops | bytes accessed | tf_op | source)
XLA Modules:
  0.0 338.0 jit_solution(14054496321634628678)
XLA Ops:
  0.6 1.2 copy.21
  1.9 0.1 reshape.33.x0_ref
  2.0 0.0 copy-start.1
  2.0 40.9 %mlp_forward.1 = (bf16[6,784,512]{2,1,0:T(8,128)(2,1)S(1)}, f32[6,784,2048]{2,1,0:T(8,128)}, f32[16,512]{1,0:T(8,128)S(1)}) custom-call(bf16[784,512]{1,0:T(8,128)(2,1)S(1)} %reshape.33.x0_ref, f32[6,512,2048]{2,1,0:T(8,128)} %w1_ref.5, f32[6,2048,512]{2,1,0:T(8,128)} %w2_ref.5), custom_call_target="tpu_custom_call" | custom-call | flops 19730006016 | bytes 88866816 | tf_op jit(solution)/shard_map/mlp_forward/pallas_call | solution.py:84
  43.0 2.2 copy-done
  45.2 0.0 copy-done.1
  45.2 0.5 fusion.12
  45.7 0.2 fusion.8
  45.9 0.1 eq.15
  46.0 0.1 multiply_convert_fusion
  46.1 0.6 reshape.34.head_ref
  46.7 0.3 convolution_multiply_fusion
  47.0 0.6 pad.8.dtop_ref
  47.6 207.6 %backward_sum.1 = (bf16[6,8,512,256]{3,2,1,0:T(8,128)(2,1)}, bf16[6,8,512,256]{3,2,1,0:T(8,128)(2,1)}, bf16[2,4,4,4,16,384]{5,4,3,2,1,0:T(8,128)(2,1)}, bf16[6,8...) custom-call(f32[8,512]{1,0:T(8,128)} %pad.8.dtop_ref, bf16[6,784,512]{2,1,0:T(8,128)(2,1)} %copy-done, ...), custom_call_target="tpu_custom_call" | custom-call | flops 39460012032 | bytes 114032640 | tf_op jit(solution)/shard_map/backward_sum/pallas_call | solution.py:494
  256.5 0.6 pad_maximum_fusion.coef_ref
  257.1 0.0 copy-done.4
  257.1 0.8 reshape.32.x0_ref
  258.0 70.7 %update_forward.1 = (f32[6,512,2048]{2,1,0:T(8,128)}, f32[6,512,2048]{2,1,0:T(8,128)}, f32[6,2048,512]{2,1,0:T(8,128)}, f32[6,2048,512]{2,1,0:T(8,128)}, f32[16,512]{1,0:T(8,128)}) custom-call(f32[2]{0:T(128)} %pad_maximum_fusion.coef_ref, bf16[392,512]{1,0:T(8,128)(2,1)} %reshape.32.x0_ref, f32[6,512,2048]{2,1,0:T(8,128)} %w1_ref.5, ...), custom_call_target="tpu_custom_call" | custom-call | flops 9865003008 | bytes 226492416 | tf_op jit(solution)/shard_map/update_forward/pallas_call | solution.py:192
  328.7 0.0 copy-start.2
  328.7 3.8 %reshape.36 = bf16[512,1536]{1,0:T(8,128)(2,1)} reshape(bf16[2,4,4,4,16,384]{5,4,3,2,1,0:T(8,128)(2,1)} %get-tuple-element.24) | data formatting | bytes 3145728 | tf_op jit(solution)/shard_map/reshape | solution.py:567
  332.5 4.2 %multiply_subtract_fusion = (f32[512,1000]{0,1:T(8,128)S(1)}, f32[512,1000]{0,1:T(8,128)}) fusion(f32[512,1000]{0,1:T(8,128)S(1)} %copy-done.2, f32[]{:T(128)} %copy.22, bf16[512,1536]{1,0:T(8,128)(2,1)} %reshape.36, f32[512,1000]{0,1:T(8,128)} %param.19, f32[]{:T(128)} %copy.23), kind=kOutput, calls=%fused_computation | convolution fusion | flops 526336000 | bytes 9764872 | tf_op jit(solution)/shard_map/bd,bc->dc/dot_general | solution.py:568
  336.7 0.0 copy-done.5
  336.7 1.3 fusion.1
  338.0 0.0 copy-done.3
  (10 shorter events, 0.1 us)
Async XLA Ops:
  2.0 43.2 %copy-start.1 = (f32[512,1000]{0,1:T(8,128)S(1)}, f32[512,1000]{0,1:T(8,128)}, u32[]{:S(2)}) copy-start(f32[512,1000]{0,1:T(8,128)} %param.16) | copy-start | bytes 6144004
  43.0 2.2 copy-start
  45.2 0.7 copy-start.6
  47.6 209.5 %copy-start.4 = (bf16[2,196,512]{2,0,1:T(2,128)(2,1)S(1)}, bf16[2,196,512]{2,0,1:T(2,128)(2,1)}, u32[]{:S(2)}) copy-start(bf16[2,196,512]{2,0,1:T(2,128)(2,1)} %param.13) | copy-start | bytes 1204228
  328.7 3.9 %copy-start.2 = (f32[512,1000]{0,1:T(8,128)S(1)}, f32[512,1000]{0,1:T(8,128)}, u32[]{:S(2)}) copy-start(f32[512,1000]{0,1:T(8,128)} %param.16) | copy-start | bytes 6144004
  332.5 4.2 %copy-start.5 = (f32[16,512]{1,0:T(8,128)S(1)}, f32[16,512]{1,0:T(8,128)}, u32[]{:S(2)}) copy-start(f32[16,512]{1,0:T(8,128)} %get-tuple-element.23) | copy-start | bytes 98308
  336.7 1.3 copy-start.3

commit v4 on v2

--- a/solution.py
+++ b/solution.py
@@ -12,7 +12,7 @@
 GELU_B = 0.044715
 CHUNK = 512
 UPD_CHUNK = 1024
-FWD_CHUNK = 1024
+FWD_CHUNK = 2048
 RING = 4
 LANES = 256
 MESH_ID = pl.DeviceIdType.MESH
@@ -101,7 +101,7 @@
         ],
         scratch_shapes=[pltpu.VMEM((rows, d), BF16), pltpu.VMEM((rows, d), BF16), pltpu.VMEM((rows, d), F32)],
         cost_estimate=cost(4 * layers * rows * d * ff, 8 * layers * d * ff + 4 * layers * rows * ff),
-        compiler_params=pltpu.CompilerParams(vmem_limit_bytes=48 << 20),
+        compiler_params=pltpu.CompilerParams(vmem_limit_bytes=62 << 20),
         name="mlp_forward",
     )(x0, w_in, w_out)
 
@@ -176,7 +176,7 @@
             pltpu.VMEM((rows, d), F32),
         ],
         cost_estimate=cost(8 * count * rows * d * ff, count * (12 * d * ff + 4 * rows * ff)),
-        compiler_params=pltpu.CompilerParams(vmem_limit_bytes=56 << 20),
+        compiler_params=pltpu.CompilerParams(vmem_limit_bytes=62 << 20),
         name="mlp_backward",
     )(d_top, xs, pre, w_in, w_out)
 
@@ -366,17 +366,14 @@
         return pltpu.make_async_copy(work.at[m, blocks], o_ref.at[layer, blocks], out_sem.at[m, slot])
 
     def accumulate(dst, sources):
-        blocks, count, _ = dst.shape
-        step = min(count, 64)
-
-        @pl.loop(0, count // step)
-        def _(r):
-            part = pl.ds(pl.multiple_of(r * step, step), step)
-            for block in range(blocks):
-                total = sources[0][block, part, :].astype(F32)
+        for block in range(dst.shape[0]):
+            if len(sources) == 2:
+                dst[block] = sources[0][block] + sources[1][block]
+            else:
+                total = sources[0][block].astype(F32)
                 for source in sources[1:]:
-                    total = total + source[block, part, :].astype(F32)
-                dst[block, part, :] = total.astype(BF16)
+                    total = total + source[block].astype(F32)
+                dst[block] = total.astype(BF16)
 
     head_way = 1 - 2 * core
 

time: 334 us -> 332 us (level)
  no operation moved by 1% of the time
where the time goes in v4:
time: 332 us
  Pallas kernels  312 us (94%)
  local copies, waits for them, and re-layouts  8.34 us (3%)
  matrix products  7.79 us (2%)
    pallas_call x1, Pallas kernels, sum_gradients(): pl.pallas_call(functools.partial(sum_body, layers), in_specs=[pl.BlockSpe...  127 us
    pallas_call x1, Pallas kernels, backward(): pl.pallas_call(functools.partial(bwd_body, n_chunk, images), grid=(count,...  76.6 us
    pallas_call x1, Pallas kernels, update_forward(): pl.pallas_call(functools.partial(next_body, n_chunk, images), grid=(layer...  70.6 us
    pallas_call x1, Pallas kernels, forward(): pl.pallas_call(functools.partial(fwd_body, n_chunk, images), grid=(layers...  37.9 us

profile of v4, /device:TPU:1, one launch (start us, length us, event | category | flops | bytes accessed | tf_op | source)
XLA Modules:
  0.0 331.9 jit_solution(12231986594458692232)
XLA Ops:
  0.6 1.2 copy.21
  1.9 1.0 reshape.36.x0_ref
  2.9 37.9 %mlp_forward.1 = (bf16[6,784,512]{2,1,0:T(8,128)(2,1)}, f32[6,784,2048]{2,1,0:T(8,128)}, f32[16,512]{1,0:T(8,128)}) custom-call(bf16[784,512]{1,0:T(8,128)(2,1)} %reshape.36.x0_ref, f32[6,512,2048]{2,1,0:T(8,128)} %w1_ref.5, f32[6,2048,512]{2,1,0:T(8,128)} %w2_ref.5), custom_call_target="tpu_custom_call" | custom-call | flops 19730006016 | bytes 88866816 | tf_op jit(solution)/shard_map/mlp_forward/pallas_call | solution.py:84
  40.8 0.9 multiply_convert_fusion.1
  41.7 2.1 fusion.12
  43.7 0.2 fusion.8
  43.9 0.0 copy-done.5
  43.9 0.1 eq.15
  44.0 0.1 multiply_convert_fusion
  44.1 0.3 convolution_multiply_fusion
  44.4 0.6 pad.8.dtop_ref
  45.0 76.6 %mlp_backward.1 = (bf16[6,8,512,256]{3,2,1,0:T(8,128)(2,1)}, bf16[6,2,4,512,256]{4,3,2,1,0:T(8,128)(2,1)}) custom-call(f32[8,512]{1,0:T(8,128)} %pad.8.dtop_ref, bf16[6,784,512]{2,1,0:T(8,128)(2,1)} %get-tuple-element.21.xs_ref, f32[6,784,2048]{2,1,0:T(8,128)} %get-tuple-element.22.pre_ref, f32[6,512,2048]{2,1,0:T(8,128)} %w1_ref.5, f32[6,2048,512]{2,1,0:T(8,128)} %w2_ref.5), custom_call_target="tpu_custom_call" | custom-call | flops 39460012032 | bytes 114032640 | tf_op jit(solution)/shard_map/mlp_backward/pallas_call | solution.py:154
  121.6 0.6 reshape.38.head_ref
  122.2 126.9 %gradient_sum.1 = (bf16[6,8,512,256]{3,2,1,0:T(8,128)(2,1)}, bf16[6,8,512,256]{3,2,1,0:T(8,128)(2,1)}, bf16[2,4,4,4,16,384]{5,4,3,2,1,0:T(8,128)(2,1)}) custom-call(bf16[6,8,512,256]{3,2,1,0:T(8,128)(2,1)} %get-tuple-element.23.g1_ref, bf16[6,8,512,256]{3,2,1,0:T(8,128)(2,1)} %bitcast.11, bf16[16,384]{1,0:T(8,128)(2,1)} %reshape.38.head_ref), custom_call_target="tpu_custom_call" | custom-call | flops 1073741824 | bytes 25165824 | tf_op jit(solution)/shard_map/gradient_sum/pallas_call | solution.py:476
  250.4 0.6 pad_maximum_fusion.coef_ref
  251.0 0.0 copy-done.3
  251.0 0.8 reshape.35.x0_ref
  251.9 70.6 %update_forward.1 = (f32[6,512,2048]{2,1,0:T(8,128)}, f32[6,512,2048]{2,1,0:T(8,128)}, f32[6,2048,512]{2,1,0:T(8,128)}, f32[6,2048,512]{2,1,0:T(8,128)}, f32[16,512]{1,0:T(8,128)}) custom-call(f32[2]{0:T(128)} %pad_maximum_fusion.coef_ref, bf16[392,512]{1,0:T(8,128)(2,1)} %reshape.35.x0_ref, f32[6,512,2048]{2,1,0:T(8,128)} %w1_ref.5, ...), custom_call_target="tpu_custom_call" | custom-call | flops 9865003008 | bytes 226492416 | tf_op jit(solution)/shard_map/update_forward/pallas_call | solution.py:226
  322.5 0.0 copy-start.1
  322.5 3.8 %reshape.40 = bf16[512,1536]{1,0:T(8,128)(2,1)} reshape(bf16[2,4,4,4,16,384]{5,4,3,2,1,0:T(8,128)(2,1)} %get-tuple-element.28) | data formatting | bytes 3145728 | tf_op jit(solution)/shard_map/reshape | solution.py:540
  326.4 0.0 copy-done.1
  326.4 4.2 %multiply_subtract_fusion = (f32[512,1000]{0,1:T(8,128)S(1)}, f32[512,1000]{0,1:T(8,128)}) fusion(f32[512,1000]{0,1:T(8,128)S(1)} %copy-done.1, f32[]{:T(128)} %copy.22, bf16[512,1536]{1,0:T(8,128)(2,1)} %reshape.40, f32[512,1000]{0,1:T(8,128)} %param.19, f32[]{:T(128)} %copy.23), kind=kOutput, calls=%fused_computation | convolution fusion | flops 526336000 | bytes 9764872 | tf_op jit(solution)/shard_map/bd,bc->dc/dot_general | solution.py:541
  330.6 1.3 fusion.1
  331.8 0.0 copy-done.2
  (9 shorter events, 0.1 us)
Async XLA Ops:
  40.8 3.2 copy-start.5
  40.8 3.3 %copy-start = (f32[512,1000]{0,1:T(8,128)S(1)}, f32[512,1000]{0,1:T(8,128)}, u32[]{:S(2)}) copy-start(f32[512,1000]{0,1:T(8,128)} %param.16) | copy-start | bytes 6144004
  122.2 128.8 %copy-start.3 = (bf16[2,196,512]{2,0,1:T(2,128)(2,1)S(1)}, bf16[2,196,512]{2,0,1:T(2,128)(2,1)}, u32[]{:S(2)}) copy-start(bf16[2,196,512]{2,0,1:T(2,128)(2,1)} %param.13) | copy-start | bytes 1204228
  322.5 3.9 %copy-start.1 = (f32[512,1000]{0,1:T(8,128)S(1)}, f32[512,1000]{0,1:T(8,128)}, u32[]{:S(2)}) copy-start(f32[512,1000]{0,1:T(8,128)} %param.16) | copy-start | bytes 6144004
  326.4 4.2 %copy-start.4 = (f32[16,512]{1,0:T(8,128)S(1)}, f32[16,512]{1,0:T(8,128)}, u32[]{:S(2)}) copy-start(f32[16,512]{1,0:T(8,128)} %get-tuple-element.27) | copy-start | bytes 98308
  330.6 1.3 copy-start.2
